TPU v7x, 128 devices: a whole 4x4x4 slice. The times are simulated.
128 devices in a mesh: dp: 4 (over z_hi, core), ctx: 32 (over z_lo, x, y).
Axes of the slice: x: 4, y: 4, z: 4 (z_hi: 2, z_lo: 2; z = z_hi * 2 + z_lo), core: 2. Of those that a mesh axis runs over, the one named last changes fastest.
Arguments:
- tokens: bfloat16 [16384, 1792], P(('dp', 'ctx')), may hold values from -24 to 24
- cotangent: bfloat16 [16384, 1792], P(('dp', 'ctx')), may hold values from -6 to 6
- expert_ids: int32 [16384, 4], P(('dp', 'ctx')), may hold values from 0 to 63, all different within a row; in each aligned block of 128 rows (0 to 127, 128 to 255, ...) at most 10 rows name the same one
- norm_gain: float32 [1792], replicated, may hold values from 0.5 to 1.5
- router_weight: bfloat16 [1792, 64], replicated, may hold values from -0.125 to 0.125
- gate_weight: bfloat16 [64, 1792, 1536], P('ctx', None, 'dp'), may hold values from -0.125 to 0.125
- up_weight: bfloat16 [64, 1792, 1536], P('ctx', None, 'dp'), may hold values from -0.125 to 0.125
- down_weight: bfloat16 [64, 1536, 1792], P('ctx', 'dp'), may hold values from -0.15625 to 0.15625
Outputs:
- grad_tokens: bfloat16 [16384, 1792], P(('dp', 'ctx'))
- grad_gate: bfloat16 [64, 1792, 1536], P('ctx', None, 'dp')
- grad_up: bfloat16 [64, 1792, 1536], P('ctx', None, 'dp')
- grad_down: bfloat16 [64, 1536, 1792], P('ctx', 'dp')
- grad_router: float32 [1792, 64], P(('dp', 'ctx'))
- grad_gain: float32 [1792], P(('dp', 'ctx'))
Inputs may be any that keep to these rules, and one draw needn't show every extreme that they name: `expert_ids`: each row names 4 different experts; among the rows of one device no expert is named more than 10 times.
All inputs are finite; a program needn't handle non-finite values.
Results may differ from a plain program's by a relative error of at most 0.02.
Values may be sent and summed in bfloat16 or wider, within the bound.
A program may use at most 192 MiB of HBM per device.

v0:
```python
import jax
import jax.numpy as jnp
from jax import lax
from jax.sharding import PartitionSpec as P

EPSILON = 1e-05
SWISH_SCALE = 1.702


def expert_pass(rows, upstream, weight, gate_weight, up_weight, down_weight):
    gate_pre = jnp.einsum("prd,pdf->prf", rows, gate_weight, preferred_element_type=jnp.float32)
    up_pre = jnp.einsum("prd,pdf->prf", rows, up_weight, preferred_element_type=jnp.float32)
    squash = jax.nn.sigmoid(SWISH_SCALE * gate_pre)
    hidden = (gate_pre * squash * (up_pre + 1.0)).astype(jnp.bfloat16)
    grad_out = jnp.einsum("prd,pfd->prf", upstream, down_weight, preferred_element_type=jnp.float32)
    score = jnp.sum(grad_out * hidden.astype(jnp.float32), axis=2)
    grad_hidden = weight[:, :, None] * grad_out
    slope = squash + SWISH_SCALE * gate_pre * squash * (1.0 - squash)
    grad_pre_gate = (grad_hidden * (up_pre + 1.0) * slope).astype(jnp.bfloat16)
    grad_pre_up = (grad_hidden * gate_pre * squash).astype(jnp.bfloat16)
    scaled_up = (weight[:, :, None] * upstream.astype(jnp.float32)).astype(jnp.bfloat16)
    down_grad = jnp.einsum(
        "prf,prd->pfd", hidden, scaled_up, preferred_element_type=jnp.float32
    ).astype(jnp.bfloat16)
    gate_grad = jnp.einsum(
        "prd,prf->pdf", rows, grad_pre_gate, preferred_element_type=jnp.float32
    ).astype(jnp.bfloat16)
    up_grad = jnp.einsum(
        "prd,prf->pdf", rows, grad_pre_up, preferred_element_type=jnp.float32
    ).astype(jnp.bfloat16)
    back = jnp.einsum(
        "prf,pdf->prd", grad_pre_gate, gate_weight, preferred_element_type=jnp.float32
    )
    back = back + jnp.einsum(
        "prf,pdf->prd", grad_pre_up, up_weight, preferred_element_type=jnp.float32
    )
    return (gate_grad, up_grad, down_grad, back, score)


def body(
    tokens, cotangent, expert_ids, norm_gain, router_weight, gate_weight, up_weight, down_weight
):
    ctx_size = lax.axis_size("ctx")
    local = gate_weight.shape[0]
    experts = router_weight.shape[1]
    rows_here = tokens.shape[0]
    picks = expert_ids.shape[1]
    width = tokens.shape[1]
    assigned = rows_here * picks
    capacity = max(2, rows_here * picks * 5 // (4 * experts))
    slots = experts * capacity
    widened = tokens.astype(jnp.float32)
    inverse = lax.rsqrt(jnp.mean(widened * widened, axis=1, keepdims=True) + EPSILON)
    scaled = widened * inverse
    normed = (scaled * norm_gain).astype(jnp.bfloat16)
    logits = jnp.dot(normed, router_weight, preferred_element_type=jnp.float32)
    labels = jnp.arange(experts, dtype=jnp.int32)
    member = expert_ids[:, :, None] == labels
    chosen = jnp.sum(jnp.where(member, logits[:, None, :], 0.0), axis=2)
    lifted = jnp.exp(chosen)
    gates = lifted / jnp.sum(lifted, axis=1, keepdims=True)
    hits = member.reshape(assigned, experts).astype(jnp.int32)
    rank = jnp.sum((jnp.cumsum(hits, axis=0) - 1) * hits, axis=1)
    position = expert_ids.reshape(-1) * capacity + rank
    match = (jnp.arange(slots, dtype=jnp.int32)[:, None] == position[None, :]).astype(jnp.float32)
    dispatch = jnp.sum(match.reshape(slots, rows_here, picks), axis=2)
    dispatch_low = dispatch.astype(jnp.bfloat16)
    out_rows = jnp.dot(dispatch_low, normed, preferred_element_type=jnp.float32).astype(
        jnp.bfloat16
    )
    out_rows = out_rows.reshape(ctx_size, local, capacity, width)
    out_grad = jnp.dot(dispatch_low, cotangent, preferred_element_type=jnp.float32).astype(
        jnp.bfloat16
    )
    out_grad = out_grad.reshape(ctx_size, local, capacity, width)
    out_gate = jnp.dot(match, gates.reshape(-1))
    out_gate = out_gate.reshape(ctx_size, local, capacity)
    arrived = (
        lax.all_to_all(out_rows, "ctx", split_axis=0, concat_axis=2, tiled=True),
        lax.all_to_all(out_grad, "ctx", split_axis=0, concat_axis=2, tiled=True),
        lax.all_to_all(
            out_gate.astype(jnp.bfloat16), "ctx", split_axis=0, concat_axis=2, tiled=True
        ).astype(out_gate.dtype),
    )
    rows, upstream, weight = (
        lax.all_gather(arrived[0], "dp", axis=2, tiled=True),
        lax.all_gather(arrived[1], "dp", axis=2, tiled=True),
        lax.all_gather(arrived[2].astype(jnp.bfloat16), "dp", axis=2, tiled=True).astype(
            jnp.float32
        ),
    )
    gate_grad, up_grad, down_grad, back, score = expert_pass(
        rows[0], upstream[0], weight[0], gate_weight, up_weight, down_weight
    )
    back_mine, score_mine = (
        lax.psum_scatter(back.astype(jnp.bfloat16), "dp", scatter_dimension=1, tiled=True).astype(
            jnp.float32
        ),
        lax.psum_scatter(score.astype(jnp.bfloat16), "dp", scatter_dimension=1, tiled=True).astype(
            jnp.float32
        ),
    )
    back_slots, score_slots = (
        lax.all_to_all(
            back_mine.astype(jnp.bfloat16), "ctx", split_axis=1, concat_axis=0, tiled=True
        ).astype(back_mine.dtype),
        lax.all_to_all(
            score_mine.astype(jnp.bfloat16), "ctx", split_axis=1, concat_axis=0, tiled=True
        ).astype(score_mine.dtype),
    )
    back_flat = back_slots.reshape(slots, width)
    score_flat = score_slots.reshape(slots)
    grad_tok = jnp.dot(dispatch.T, back_flat)
    score_tok = jnp.dot(score_flat, match).reshape(rows_here, picks)
    mixed = jnp.sum(gates * score_tok, axis=1, keepdims=True)
    grad_chosen = gates * (score_tok - mixed)
    grad_logits = jnp.sum(jnp.where(member, grad_chosen[:, :, None], 0.0), axis=1).astype(
        jnp.bfloat16
    )
    grad_normed = grad_tok + jnp.dot(
        grad_logits, router_weight.T, preferred_element_type=jnp.float32
    )
    router_part = jnp.dot(normed.T, grad_logits, preferred_element_type=jnp.float32)
    gain_part = jnp.sum(grad_normed * scaled, axis=0)
    router_grad, gain_grad = (
        lax.psum_scatter(router_part, ("dp", "ctx"), scatter_dimension=0, tiled=True),
        lax.psum_scatter(gain_part, ("dp", "ctx"), scatter_dimension=0, tiled=True),
    )
    grad_scaled = grad_normed * norm_gain
    correction = jnp.mean(grad_scaled * scaled, axis=1, keepdims=True)
    grad_input = (
        cotangent.astype(jnp.float32) + inverse * (grad_scaled - scaled * correction)
    ).astype(jnp.bfloat16)
    return (grad_input, gate_grad, up_grad, down_grad, router_grad, gain_grad)


def solution(mesh):
    return jax.shard_map(
        body,
        mesh=mesh,
        in_specs=(
            P(("dp", "ctx"), None),
            P(("dp", "ctx"), None),
            P(("dp", "ctx"), None),
            P(),
            P(),
            P("ctx", None, "dp"),
            P("ctx", None, "dp"),
            P("ctx", "dp", None),
        ),
        out_specs=(
            P(("dp", "ctx"), None),
            P("ctx", None, "dp"),
            P("ctx", None, "dp"),
            P("ctx", "dp", None),
            P(("dp", "ctx"), None),
            P(("dp", "ctx")),
        ),
        check_vma=False,
    )
```

profile of v0, /device:TPU:1, one launch (start us, length us, event | category | flops | bytes accessed | tf_op | source)
XLA Modules:
  0.0 854.9 jit_solution(9014192209533966569)
XLA Ops:
  15.5 5.2 reshape.145
  20.7 3.8 copy.111
  24.5 38.7 %all_to_all.85 = bf16[32,2,10,1792]{3,1,2,0:T(2,128)(2,1)S(1)} all-to-all(bf16[32,2,10,1792]{3,1,2,0:T(2,128)(2,1)S(1)} %copy.111), channel_id=1, replica_groups=mesh['dp'=4,'ctx'=32] {'ctx'}, dimensions={0} | all-to-all | bytes 4587520 | tf_op jit(solution)/shard_map/all_to_all | solution.py:79
  67.1 5.2 reshape.144
  72.3 4.1 copy.109
  76.4 33.0 %all_to_all.86 = bf16[32,2,10,1792]{3,1,2,0:T(2,128)(2,1)S(1)} all-to-all(bf16[32,2,10,1792]{3,1,2,0:T(2,128)(2,1)S(1)} %copy.109), channel_id=1, replica_groups=mesh['dp'=4,'ctx'=32] {'ctx'}, dimensions={0} | all-to-all | bytes 4587520 | tf_op jit(solution)/shard_map/all_to_all | solution.py:80
  114.7 42.2 %all-gather.5.cloned.1.call-done = bf16[1,2,1280,1792]{3,2,1,0:T(8,128)(2,1)} async-done(((bf16[1,2,320,1792]{3,2,1,0:T(8,128)(2,1)}), bf16[1,2,1280,1792]{3,2,1,0:T(8,128)(2,1)}) %all-gather.5.cloned.1.call-update) | async-done | bytes 9175056 | tf_op jit(solution)/shard_map/all_gather | solution.py:86
  156.9 9.4 %fusion.6 = f32[2,1280,384]{1,2,0:T(8,128)} fusion(bf16[2,1792,384]{2,1,0:T(8,128)(2,1)S(1)} %copy-done, bf16[1,2,1280,1792]{3,2,1,0:T(8,128)(2,1)} %all-gather.5.cloned.1.call-done), kind=kOutput, calls=%fused_computation.7 | convolution fusion | flops 3523215360 | bytes 15859712 | tf_op jit(solution)/shard_map/prd,pdf->prf/dot_general | solution.py:11
  166.3 10.8 %fusion.14 = f32[2,1280,384]{1,2,0:T(8,128)} fusion(bf16[2,1792,384]{2,1,0:T(8,128)(2,1)S(1)} %copy-done.4, bf16[1,2,1280,1792]{3,2,1,0:T(8,128)(2,1)} %all-gather.5.cloned.1.call-done), kind=kOutput, calls=%fused_computation.15 | convolution fusion | flops 3524198400 | bytes 15859712 | tf_op jit(solution)/shard_map/prd,pdf->prf/dot_general | solution.py:12
  177.1 48.2 %all-gather.3.cloned.1.call-done = bf16[1,2,1280,1792]{3,2,1,0:T(8,128)(2,1)} async-done(((bf16[1,2,320,1792]{3,2,1,0:T(8,128)(2,1)}), bf16[1,2,1280,1792]{3,2,1,0:T(8,128)(2,1)}) %all-gather.3.cloned.1.call-update) | async-done | bytes 9175056 | tf_op jit(solution)/shard_map/all_gather | solution.py:87
  225.3 13.1 %multiply_reduce_fusion = (bf16[2,1280]{1,0:T(2,128)(2,1)S(1)}, bf16[2,1280,384]{1,2,0:T(8,128)(2,1)}, f32[2,1280,384]{1,2,0:T(8,128)}) fusion(f32[2,1280,384]{1,2,0:T(8,128)} %fusion.14, f32[2,1280,384]{1,2,0:T(8,128)} %fusion.6, bf16[2,384,1792]{2,1,0:T(8,128)(2,1)} %param.15, bf16[1,2,1280,1792]{3,2,1,0:T(8,128)(2,1)} %all-gather.3.cloned.1.call-done), kind=kOutput, calls=%fused_computation.16 | convolution fusion | flops 3533043200 | bytes 25695232 | tf_op jit(solution)/shard_map/prd,pfd->prf/dot_general | solution.py:15
  239.4 26.2 %reduce-scatter.9.cloned.1.call-done = bf16[320,2]{1,0:T(8,128)(2,1)} async-done(((bf16[1280,2]{1,0:T(8,128)(2,1)}), bf16[320,2]{1,0:T(8,128)(2,1)}) %reduce-scatter.9.cloned.1.call-update) | async-done | bytes 1296
  267.3 6.9 all-to-all-start.4
  276.4 5.0 all-to-all-done.4
  285.6 10.2 %all_to_all.87 = bf16[32,2,10]{2,1,0:T(2,128)(2,1)S(1)} all-to-all(bf16[32,2,10]{2,1,0:T(2,128)(2,1)S(1)} %bitcast.98), channel_id=1, replica_groups=mesh['dp'=4,'ctx'=32] {'ctx'}, dimensions={0} | all-to-all | bytes 2560 | tf_op jit(solution)/shard_map/all_to_all | solution.py:81
  297.3 11.9 %all_gather.9 = bf16[1,2,1280]{1,0,2:T(2,128)(2,1)S(1)} all-gather(bf16[1,2,320]{1,0,2:T(2,128)(2,1)S(1)} %copy.107), channel_id=1, replica_groups=mesh['dp'=4,'ctx'=32] {'dp'}, dimensions={2}, use_global_device_ids=true | all-gather | bytes 6400 | tf_op jit(solution)/shard_map/all_gather | solution.py:88
  311.9 6.4 multiply_convert_fusion.3
  318.3 9.2 %fusion.51 = f32[2,1280,1792]{2,1,0:T(8,128)} fusion(bf16[2,1280,384]{1,2,0:T(8,128)(2,1)S(1)} %get-tuple-element.13, bf16[2,1792,384]{2,1,0:T(8,128)(2,1)S(1)} %copy-done), kind=kOutput, calls=%fused_computation.77 | convolution fusion | flops 3523215360 | bytes 23068672 | tf_op jit(solution)/shard_map/prf,pdf->prd/dot_general | solution.py:31
  327.5 16.4 %add_convert_fusion = bf16[2,1280,1792]{2,1,0:T(8,128)(2,1)} fusion(f32[2,1280,1792]{2,1,0:T(8,128)} %fusion.51, bf16[2,1280,384]{1,2,0:T(8,128)(2,1)} %get-tuple-element.12, bf16[2,1792,384]{2,1,0:T(8,128)(2,1)} %param.14), kind=kOutput, calls=%fused_computation.1 | convolution fusion | flops 3532390400 | bytes 32243712 | tf_op jit(solution)/shard_map/prf,pdf->prd/dot_general | solution.py:34
  345.0 284.2 %fusion = f32[16,64]{1,0:T(8,128)S(1)} fusion(f32[1792,64]{1,0:T(8,128)S(1)} %fusion.43), kind=kCustom, calls=%all-reduce-scatter | all-reduce-scatter fusion | flops 131073 | bytes 462848
  633.1 25.5 %collective-permute-start.13 = (f32[16,64]{1,0:T(8,128)S(1)}, f32[16,64]{1,0:T(8,128)S(1)}, u32[]{:S(2)}, u32[]{:S(2)}) collective-permute-start(f32[16,64]{1,0:T(8,128)S(1)} %fusion), channel_id=1, source_target_pairs={{0,14},{1,15},{2,16},{3,17},{4,18},{5,19},{6,20},{7,21},{8,22},{9,... | collective-permute-start | bytes 12296
  662.6 5.4 copy.117
  668.0 21.9 %all-to-all-start.3 = ((bf16[2,320,1792]{2,0,1:T(2,128)(2,1)}), bf16[2,320,1792]{2,0,1:T(2,128)(2,1)S(1)}, u32[]{:S(2)}, u32[]{:S(2)}) async-start(bf16[2,320,1792]{2,0,1:T(2,128)(2,1)} %copy.117), calls=%async_computation.4 | async-start | bytes 4587520 | tf_op jit(solution)/shard_map/all_to_all | solution.py:104
  689.9 6.8 collective-permute-start.10
  696.7 9.6 %fusion.17 = bf16[2,384,1792]{2,1,0:T(8,128)(2,1)} fusion(bf16[2,1280,384]{1,2,0:T(8,128)(2,1)} %get-tuple-element.11, bf16[1,2,1280,1792]{3,2,1,0:T(8,128)(2,1)} %all-gather.3.cloned.1.call-done, f32[2,1280]{1,0:T(2,128)S(1)} %copy.108), kind=kOutput, calls=%fused_computation.21 | convolution fusion | flops 3538354176 | bytes 13903872 | tf_op jit(solution)/shard_map/prf,prd->pfd/dot_general | solution.py:22
  709.7 4.7 collective-permute-start.8
  719.8 4.3 collective-permute-start.5
  724.1 12.0 %fusion.21 = bf16[2,1792,384]{2,1,0:T(8,128)(2,1)} fusion(bf16[2,1280,384]{1,2,0:T(8,128)(2,1)} %get-tuple-element.12, bf16[1,2,1280,1792]{3,2,1,0:T(8,128)(2,1)} %all-gather.5.cloned.1.call-done), kind=kOutput, calls=%fused_computation.23 | convolution fusion | flops 3524591616 | bytes 13893632 | tf_op jit(solution)/shard_map/prd,prf->pdf/dot_general | solution.py:28
  742.7 6.4 collective-permute-start.2
  753.7 12.0 %fusion.18 = bf16[2,1792,384]{2,1,0:T(8,128)(2,1)} fusion(bf16[2,1280,384]{1,2,0:T(8,128)(2,1)} %copy-done.3, bf16[1,2,1280,1792]{3,2,1,0:T(8,128)(2,1)} %all-gather.5.cloned.1.call-done), kind=kOutput, calls=%fused_computation.22 | convolution fusion | flops 3524591616 | bytes 13893632 | tf_op jit(solution)/shard_map/prd,prf->pdf/dot_general | solution.py:25
  770.6 5.5 reshape.146
  780.5 64.6 %all-reduce.1 = f32[1792]{0:T(1024)S(1)} all-reduce(f32[1792]{0:T(1024)S(1)} %get-tuple-element.6), channel_id=5, replica_groups=mesh['dp'=4,'ctx'=32] {'dp','ctx'}, use_global_device_ids=true, to_apply=%region_15.16.clone | all-reduce | flops 1792 | bytes 14336
  (120 shorter events, 72.0 us)
Async XLA Ops:
  7.2 149.7 %copy-start = (bf16[2,1792,384]{2,1,0:T(8,128)(2,1)S(1)}, bf16[2,1792,384]{2,1,0:T(8,128)(2,1)}, u32[]{:S(2)}) copy-start(bf16[2,1792,384]{2,1,0:T(8,128)(2,1)} %param.13) | copy-start | bytes 8257540
  7.2 149.7 %all-gather.5.cloned.1.call-start = ((), (), s32[]{:S(2)}) async-start(), calls=%async_computation.8 | async-start | bytes 11468800 | tf_op jit(solution)/shard_map/all_gather | solution.py:86
  9.6 103.8 %copy-start.10 = (f32[128]{0:T(128)}, f32[128]{0:T(128)S(1)}, u32[]{:S(2)}) copy-start(f32[128]{0:T(128)S(1)} %add_rsqrt_fusion) | copy-start | bytes 1540
  63.3 1.7 copy-start.5
  64.9 160.4 %all-gather.3.cloned.1.call-start = ((), (), s32[]{:S(2)}) async-start(), calls=%async_computation.7 | async-start | bytes 11468800 | tf_op jit(solution)/shard_map/all_gather | solution.py:87
  109.4 4.0 copy-start.2
  109.4 4.0 copy-start.6
  111.0 154.6 %reduce-scatter.9.cloned.1.call-start = ((), (), s32[]{:S(2)}) async-start(), calls=%async_computation.10 | async-start | bytes 409600
  156.9 9.4 %copy-start.4 = (bf16[2,1792,384]{2,1,0:T(8,128)(2,1)S(1)}, bf16[2,1792,384]{2,1,0:T(8,128)(2,1)}, u32[]{:S(2)}) copy-start(bf16[2,1792,384]{2,1,0:T(8,128)(2,1)} %param.14) | copy-start | bytes 8257540
  177.1 62.3 %copy-start.7 = (s32[128,4]{0,1:T(4,128)S(1)}, s32[128,4]{0,1:T(4,128)}, u32[]{:S(2)}) copy-start(s32[128,4]{0,1:T(4,128)} %param.10) | copy-start | bytes 6148
  267.3 14.1 %all-to-all-start.4 = ((bf16[2,32,10]{2,0,1:T(2,128)(2,1)}), bf16[2,32,10]{2,0,1:T(2,128)(2,1)S(1)}, u32[]{:S(2)}, u32[]{:S(2)}) async-start(bf16[2,32,10]{2,0,1:T(2,128)(2,1)} %copy.119), calls=%async_computation.5 | async-start | bytes 32768 | tf_op jit(solution)/shard_map/all_to_all | solution.py:107
  274.3 388.4 %reduce-scatter.7.cloned.1.call-start = ((), (), s32[]{:S(2)}) async-start(), calls=%async_computation.9 | async-start | bytes 11468800 | tf_op jit(solution)/shard_map/reduce_scatter | solution.py:96
  283.6 12.1 %copy-start.8 = (f32[128,4]{0,1:T(4,128)}, f32[128,4]{0,1:T(4,128)S(1)}, u32[]{:S(2)}) copy-start(f32[128,4]{0,1:T(4,128)S(1)} %get-tuple-element.9) | copy-start | bytes 6148
  318.3 9.2 %copy-start.3 = (bf16[2,1280,384]{1,2,0:T(8,128)(2,1)}, bf16[2,1280,384]{1,2,0:T(8,128)(2,1)S(1)}, u32[]{:S(2)}) copy-start(bf16[2,1280,384]{1,2,0:T(8,128)(2,1)S(1)} %get-tuple-element.13) | copy-start | bytes 5898244
  629.2 60.7 %collective-permute-start.15 = (f32[14,64]{1,0:T(8,128)S(1)}, f32[14,64]{1,0:T(8,128)S(1)}, u32[]{:S(2)}, u32[]{:S(2)}) collective-permute-start(f32[14,64]{1,0:T(8,128)S(1)} %slice.9), channel_id=1, source_target_pairs={{0,16},{1,17},{2,18},{3,19},{4,20},{5,21},{6,22},{7,23},{8,24},{9,... | collective-permute-start | bytes 10760
  631.1 75.1 %collective-permute-start.14 = (f32[16,64]{1,0:T(8,128)S(1)}, f32[16,64]{1,0:T(8,128)S(1)}, u32[]{:S(2)}, u32[]{:S(2)}) collective-permute-start(f32[16,64]{1,0:T(8,128)S(1)} %fusion), channel_id=1, source_target_pairs={{0,15},{1,16},{2,17},{3,18},{4,19},{5,20},{6,21},{7,22},{8,23},{9,... | collective-permute-start | bytes 12296
  633.1 76.6 %collective-permute-start.13 = (f32[16,64]{1,0:T(8,128)S(1)}, f32[16,64]{1,0:T(8,128)S(1)}, u32[]{:S(2)}, u32[]{:S(2)}) collective-permute-start(f32[16,64]{1,0:T(8,128)S(1)} %fusion), channel_id=1, source_target_pairs={{0,14},{1,15},{2,16},{3,17},{4,18},{5,19},{6,20},{7,21},{8,22},{9,... | collective-permute-start | bytes 12296
  658.6 55.8 %collective-permute-start.12 = (f32[16,64]{1,0:T(8,128)S(1)}, f32[16,64]{1,0:T(8,128)S(1)}, u32[]{:S(2)}, u32[]{:S(2)}) collective-permute-start(f32[16,64]{1,0:T(8,128)S(1)} %fusion), channel_id=1, source_target_pairs={{0,13},{1,14},{2,15},{3,16},{4,17},{5,18},{6,19},{7,20},{8,21},{9,... | collective-permute-start | bytes 12296
  660.5 55.8 %collective-permute-start.11 = (f32[16,64]{1,0:T(8,128)S(1)}, f32[16,64]{1,0:T(8,128)S(1)}, u32[]{:S(2)}, u32[]{:S(2)}) collective-permute-start(f32[16,64]{1,0:T(8,128)S(1)} %fusion), channel_id=1, source_target_pairs={{0,12},{1,13},{2,14},{3,15},{4,16},{5,17},{6,18},{7,19},{8,20},{9,... | collective-permute-start | bytes 12296
  668.0 100.1 %all-to-all-start.3 = ((bf16[2,320,1792]{2,0,1:T(2,128)(2,1)}), bf16[2,320,1792]{2,0,1:T(2,128)(2,1)S(1)}, u32[]{:S(2)}, u32[]{:S(2)}) async-start(bf16[2,320,1792]{2,0,1:T(2,128)(2,1)} %copy.117), calls=%async_computation.4 | async-start | bytes 4587520 | tf_op jit(solution)/shard_map/all_to_all | solution.py:104
  689.9 29.9 %collective-permute-start.10 = (f32[16,64]{1,0:T(8,128)S(1)}, f32[16,64]{1,0:T(8,128)S(1)}, u32[]{:S(2)}, u32[]{:S(2)}) collective-permute-start(f32[16,64]{1,0:T(8,128)S(1)} %fusion), channel_id=1, source_target_pairs={{0,11},{1,12},{2,13},{3,14},{4,15},{5,16},{6,17},{7,18},{8,19},{9,... | collective-permute-start | bytes 12296
  706.3 29.8 %collective-permute-start.9 = (f32[16,64]{1,0:T(8,128)S(1)}, f32[16,64]{1,0:T(8,128)S(1)}, u32[]{:S(2)}, u32[]{:S(2)}) collective-permute-start(f32[16,64]{1,0:T(8,128)S(1)} %fusion), channel_id=1, source_target_pairs={{0,10},{1,11},{2,12},{3,13},{4,14},{5,15},{6,16},{7,17},{8,18},{9,... | collective-permute-start | bytes 12296
  709.7 29.2 %collective-permute-start.8 = (f32[16,64]{1,0:T(8,128)S(1)}, f32[16,64]{1,0:T(8,128)S(1)}, u32[]{:S(2)}, u32[]{:S(2)}) collective-permute-start(f32[16,64]{1,0:T(8,128)S(1)} %fusion), channel_id=1, source_target_pairs={{0,9},{1,10},{2,11},{3,12},{4,13},{5,14},{6,15},{7,16},{8,17},{9,1... | collective-permute-start | bytes 12296
  714.4 28.3 %collective-permute-start.7 = (f32[16,64]{1,0:T(8,128)S(1)}, f32[16,64]{1,0:T(8,128)S(1)}, u32[]{:S(2)}, u32[]{:S(2)}) collective-permute-start(f32[16,64]{1,0:T(8,128)S(1)} %fusion), channel_id=1, source_target_pairs={{0,8},{1,9},{2,10},{3,11},{4,12},{5,13},{6,14},{7,15},{8,16},{9,17... | collective-permute-start | bytes 12296
  716.3 32.8 %collective-permute-start.6 = (f32[16,64]{1,0:T(8,128)S(1)}, f32[16,64]{1,0:T(8,128)S(1)}, u32[]{:S(2)}, u32[]{:S(2)}) collective-permute-start(f32[16,64]{1,0:T(8,128)S(1)} %fusion), channel_id=1, source_target_pairs={{0,7},{1,8},{2,9},{3,10},{4,11},{5,12},{6,13},{7,14},{8,15},{9,16}... | collective-permute-start | bytes 12296
  719.8 31.2 %collective-permute-start.5 = (f32[16,64]{1,0:T(8,128)S(1)}, f32[16,64]{1,0:T(8,128)S(1)}, u32[]{:S(2)}, u32[]{:S(2)}) collective-permute-start(f32[16,64]{1,0:T(8,128)S(1)} %fusion), channel_id=1, source_target_pairs={{0,6},{1,7},{2,8},{3,9},{4,10},{5,11},{6,12},{7,13},{8,14},{9,15},... | collective-permute-start | bytes 12296
  736.1 29.6 %collective-permute-start.4 = (f32[16,64]{1,0:T(8,128)S(1)}, f32[16,64]{1,0:T(8,128)S(1)}, u32[]{:S(2)}, u32[]{:S(2)}) collective-permute-start(f32[16,64]{1,0:T(8,128)S(1)} %fusion), channel_id=1, source_target_pairs={{0,5},{1,6},{2,7},{3,8},{4,9},{5,10},{6,11},{7,12},{8,13},{9,14},{... | collective-permute-start | bytes 12296
  738.9 26.8 %collective-permute-start.3 = (f32[16,64]{1,0:T(8,128)S(1)}, f32[16,64]{1,0:T(8,128)S(1)}, u32[]{:S(2)}, u32[]{:S(2)}) collective-permute-start(f32[16,64]{1,0:T(8,128)S(1)} %fusion), channel_id=1, source_target_pairs={{0,4},{1,5},{2,6},{3,7},{4,8},{5,9},{6,10},{7,11},{8,12},{9,13},{1... | collective-permute-start | bytes 12296
  742.7 23.1 %collective-permute-start.2 = (f32[16,64]{1,0:T(8,128)S(1)}, f32[16,64]{1,0:T(8,128)S(1)}, u32[]{:S(2)}, u32[]{:S(2)}) collective-permute-start(f32[16,64]{1,0:T(8,128)S(1)} %fusion), channel_id=1, source_target_pairs={{0,3},{1,4},{2,5},{3,6},{4,7},{5,8},{6,9},{7,10},{8,11},{9,12},{10... | collective-permute-start | bytes 12296
  749.1 16.6 %collective-permute-start.1 = (f32[16,64]{1,0:T(8,128)S(1)}, f32[16,64]{1,0:T(8,128)S(1)}, u32[]{:S(2)}, u32[]{:S(2)}) collective-permute-start(f32[16,64]{1,0:T(8,128)S(1)} %fusion), channel_id=1, source_target_pairs={{0,2},{1,3},{2,4},{3,5},{4,6},{5,7},{6,8},{7,9},{8,10},{9,11},{10,... | collective-permute-start | bytes 12296
  751.0 14.7 %collective-permute-start = (f32[16,64]{1,0:T(8,128)S(1)}, f32[16,64]{1,0:T(8,128)S(1)}, u32[]{:S(2)}, u32[]{:S(2)}) collective-permute-start(f32[16,64]{1,0:T(8,128)S(1)} %fusion), channel_id=1, source_target_pairs={{0,1},{1,2},{2,3},{3,4},{4,5},{5,6},{6,7},{7,8},{8,9},{9,10},{10,1... | collective-permute-start | bytes 12296
  770.6 77.6 %copy-start.1 = (bf16[2,1792,384]{2,1,0:T(8,128)(2,1)S(1)}, bf16[2,1792,384]{2,1,0:T(8,128)(2,1)}, u32[]{:S(2)}) copy-start(bf16[2,1792,384]{2,1,0:T(8,128)(2,1)} %param.13) | copy-start | bytes 8257540
  (3 other events, 2.1 us)
Sparse Core Ops, SparseCore 0:
  65.0 91.8 all-gather.4
  159.2 66.1 all-gather.2
  239.5 26.0 reduce-scatter.8
  344.0 81.2 reduce-scatter.6
where the time goes:
time: 863 us; the launch traced here: 855 us
  blocking collectives  443 us (51%)
  waiting for transfers between devices  122 us (14%)
  starting transfers between devices  105 us (12%)
  matrix products  105 us (12%)
  local copies, waits for them, and re-layouts  48.2 us (6%)
  other arithmetic  18 us (2%)
  between operations  14.4 us (2%)
    unnamed x2, blocking collectives  349 us
    unnamed x17, starting transfers between devices  75.7 us
    all_gather x1, waiting for transfers between devices, body(): lax.all_gather(arrived[1], 'dp', axis=2, tiled=True)  48.2 us
    all_gather x1, waiting for transfers between devices, body(): lax.all_gather(arrived[0], 'dp', axis=2, tiled=True)  42.2 us
    all_to_all x1, blocking collectives, body(): lax.all_to_all(out_rows, 'ctx', split_axis=0, concat_axis=2, tiled=True)  38.7 us
    all_to_all x1, blocking collectives, body(): lax.all_to_all(out_grad, 'ctx', split_axis=0, concat_axis=2, tiled=True)  33 us
    unnamed x21, waiting for transfers between devices  26.3 us
    all_to_all x1, starting transfers between devices, body(): lax.all_to_all(back_mine.astype(jnp.bfloat16), 'ctx', split_axis=1, conca...  21.9 us
  transfers between devices with their start and end apart: 22, of which 4 were waited for; matrix products, arithmetic and copies ran while one was open for 43% of the time, Pallas kernels for 0%

commit v1 on v0

v1 whole, which is shorter than its diff:
```python
import functools

import jax
import jax.numpy as jnp
from jax import lax
from jax.experimental import pallas as pl
from jax.experimental.pallas import tpu as pltpu
from jax.sharding import PartitionSpec as P

EPSILON = 1e-05
SWISH_SCALE = 1.702
MESH = pl.DeviceIdType.MESH
SLOTS = 8
EXTRA = 2
ROW_BLOCK = 256
DEVICES = 128


def coordinates():
    dp, ctx = lax.axis_index("dp"), lax.axis_index("ctx")
    return (ctx // 4) % 4, ctx % 4, (dp // 2) * 2 + ctx // 16, dp % 2


def device_of(x, y, z, core):
    return (z // 2) * 2 + core, (z % 2) * 16 + x * 4 + y


def expert_of(dp, ctx):
    return 2 * ctx + dp % 2


def half_and_expert(dp, ctx):
    return (dp // 2) * 64 + expert_of(dp, ctx)


def dot(a, b, contract):
    return lax.dot_general(a, b, (contract, ((), ())), preferred_element_type=jnp.float32)


def moe_kernel(
    out_main, out_extra, gate_weight, up_weight, down_weight,
    home_main, home_extra, gate_grad, up_grad, down_grad,
    rows, back, w_gate, w_up, w_down, hid, gat, upp, gate_buf, up_buf, down_buf,
    go_send, go_recv, home_send, home_recv, local_sem, load_sem,
    weight_send, weight_recv, grad_send, grad_recv,
):
    x, y, z, core = coordinates()
    mine = device_of(x, y, z, core)
    partner = device_of(x, y, z, 1 - core)
    edge = DEVICES * SLOTS
    half = down_weight.shape[1]
    width = down_weight.shape[2]

    def turn(k, sign, flip):
        return device_of(
            (x + sign * k + DEVICES) % 4,
            (y + sign * (3 * k + k // 4) + 4 * DEVICES) % 4,
            (z + sign * (2 * k + k // 4 + k // 16) + 4 * DEVICES) % 4,
            flip,
        )

    def target(k):
        return turn(k, 1 - 2 * core, (core + k // 64 + k // 4) % 2)

    def source(k):
        other = (core + k // 64 + k // 4) % 2
        return turn(k, 2 * other - 1, other)

    def main_slot(ref, i):
        return ref.at[pl.ds(pl.multiple_of(i * SLOTS, SLOTS), SLOTS)]

    def extra_slot(ref, i, first=0):
        return ref.at[pl.ds(pl.multiple_of(first + i * EXTRA, EXTRA), EXTRA)]

    barrier = pltpu.get_barrier_semaphore()

    def greet(k, carry):
        pl.semaphore_signal(barrier, inc=1, device_id=target(k), device_id_type=MESH)
        return carry

    lax.fori_loop(1, DEVICES, greet, 0)
    pl.semaphore_wait(barrier, DEVICES - 1)

    def remote(src, dst, send, recv, device):
        return pltpu.make_async_remote_copy(
            src_ref=src, dst_ref=dst, send_sem=send, recv_sem=recv,
            device_id=device, device_id_type=MESH,
        )

    def go_main(k):
        to = target(k)
        return remote(
            main_slot(out_main, expert_of(*to)), main_slot(rows, k),
            go_send.at[0, k], go_recv.at[0, k], to,
        )

    def go_extra(k):
        to = target(k)
        return remote(
            extra_slot(out_extra, expert_of(*to)), extra_slot(rows, k, edge),
            go_send.at[1, k], go_recv.at[1, k], to,
        )

    def home_copy(k, to, index, kind):
        if kind == 0:
            src, dst = main_slot(back, k), main_slot(home_main, index)
        else:
            src, dst = extra_slot(back, k, edge), extra_slot(home_extra, index)
        return remote(src, dst, home_send.at[kind, k], home_recv.at[kind, index], to)

    own_index = half_and_expert(*mine)

    def return_main(k, carry):
        home_copy(k, source(k), own_index, 0).start()
        return carry

    def return_extra(k, carry):
        home_copy(k, source(k), own_index, 1).start()
        return carry

    places = (w_gate, w_up, w_down)

    def part(buf, i):
        at = pl.ds(i * half, half)
        return buf.at[at] if buf.shape[0] == 2 * half else buf.at[:, at]

    loads = []
    for i, (weight, place) in enumerate(zip((gate_weight, up_weight, down_weight), places)):
        loads.append(remote(
            weight.at[1 - core], part(place, 1), weight_send.at[i], weight_recv.at[i], partner
        ))
        loads.append(pltpu.make_async_copy(weight.at[core], part(place, 0), load_sem.at[i]))
    own = expert_of(*mine)
    loads.append(pltpu.make_async_copy(main_slot(out_main, own), main_slot(rows, 0), local_sem.at[0]))
    loads.append(
        pltpu.make_async_copy(extra_slot(out_extra, own), extra_slot(rows, 0, edge), local_sem.at[1])
    )

    def go(k, carry):
        go_main(k).start()
        go_extra(k).start()
        return carry

    for item in loads:
        item.start()
    lax.fori_loop(1, DEVICES, go, 0)
    for item in loads:
        item.wait()

    def main_came(k, carry):
        go_main(k).wait_recv()
        return carry

    def extra_came(k, carry):
        go_extra(k).wait_recv()
        return carry

    senders = ROW_BLOCK // SLOTS
    blocks = edge // ROW_BLOCK

    def step(i, carry):
        first = i * senders
        lax.fori_loop(jnp.maximum(first, 1), jnp.minimum(first + senders, DEVICES), main_came, 0)
        lax.fori_loop(DEVICES - (i // blocks) * (DEVICES - 1), DEVICES, extra_came, 0)
        block = pl.ds(pl.multiple_of(i * ROW_BLOCK, ROW_BLOCK), ROW_BLOCK)
        normed = rows[block, :width]
        upstream = rows[block, width:]
        gate_pre = dot(normed, w_gate[...], ((1,), (0,)))
        up_pre = dot(normed, w_up[...], ((1,), (0,))) + 1.0
        grad_hidden = dot(upstream, w_down[...], ((1,), (1,)))
        squash = jax.nn.sigmoid(SWISH_SCALE * gate_pre)
        swish = gate_pre * squash
        hidden = (swish * up_pre).astype(jnp.bfloat16)
        slope = squash + SWISH_SCALE * swish * (1.0 - squash)
        pre_gate = (grad_hidden * up_pre * slope).astype(jnp.bfloat16)
        pre_up = (grad_hidden * swish).astype(jnp.bfloat16)
        hid[block, :] = hidden
        gat[block, :] = pre_gate
        upp[block, :] = pre_up
        score = jnp.sum(grad_hidden * hidden.astype(jnp.float32), axis=1, keepdims=True)
        high = score.astype(jnp.bfloat16).astype(jnp.float32)
        lane = lax.broadcasted_iota(jnp.int32, (ROW_BLOCK, 128), 1)
        tail = jnp.where(lane == 0, high, jnp.where(lane == 1, score - high, 0.0))
        total = dot(pre_gate, w_gate[...], ((1,), (1,))) + dot(pre_up, w_up[...], ((1,), (1,)))
        back[block, :width] = total.astype(jnp.bfloat16)
        back[block, width:] = tail.astype(jnp.bfloat16)
        lax.fori_loop(jnp.maximum(first - senders, 1), first, return_main, 0)
        return carry

    lax.fori_loop(0, blocks + 1, step, 0)

    def columns(i, carry):
        at = pl.ds(pl.multiple_of(i * TILE, TILE), TILE)
        tile = rows[:, at]
        gate_buf[at, :] = dot(tile, gat[...], ((0,), (0,))).astype(jnp.bfloat16)
        up_buf[at, :] = dot(tile, upp[...], ((0,), (0,))).astype(jnp.bfloat16)
        return carry

    def units(i, carry):
        at = pl.ds(pl.multiple_of(i * TILE, TILE), TILE)
        down_buf[at, :] = dot(hid[:, at], rows[:, width:], ((0,), (0,))).astype(jnp.bfloat16)
        return carry

    lax.fori_loop(0, 1, units, 0)
    lax.fori_loop(1, DEVICES, return_extra, 0)
    kept = [
        pltpu.make_async_copy(main_slot(back, 0), main_slot(home_main, own_index), local_sem.at[0]),
        pltpu.make_async_copy(
            extra_slot(back, 0, edge), extra_slot(home_extra, own_index), local_sem.at[1]
        ),
    ]
    for item in kept:
        item.start()
    lax.fori_loop(1, 2 * half // TILE, units, 0)
    lax.fori_loop(0, width // TILE, columns, 0)
    grads = zip((down_buf, gate_buf, up_buf), (down_grad, gate_grad, up_grad))
    for i, (buf, out) in enumerate(grads):
        kept.append(remote(part(buf, 1), out.at[core], grad_send.at[i], grad_recv.at[i], partner))
        kept.append(pltpu.make_async_copy(part(buf, 0), out.at[core], load_sem.at[i]))
    for item in kept[2:]:
        item.start()

    def finish(k, carry):
        go_main(k).wait_send()
        go_extra(k).wait_send()
        index = half_and_expert(*target(k))
        for kind in range(2):
            home_copy(k, source(k), own_index, kind).wait_send()
            home_copy(k, source(k), index, kind).wait_recv()
        return carry

    lax.fori_loop(1, DEVICES, finish, 0)
    for item in kept:
        item.wait()


TILE = 256


def moe(out_main, out_extra, weights):
    half, width = weights[2].shape[1:]
    units = 2 * half
    count = DEVICES * (SLOTS + EXTRA)
    low = jnp.bfloat16
    anywhere = pl.BlockSpec(memory_space=pl.ANY)
    pair = pltpu.SemaphoreType.DMA((2, DEVICES))
    three = pltpu.SemaphoreType.DMA((3,))
    return pl.pallas_call(
        moe_kernel,
        out_shape=[
            jax.ShapeDtypeStruct((DEVICES * SLOTS, width + 128), low),
            jax.ShapeDtypeStruct((DEVICES * EXTRA, width + 128), low),
            jax.ShapeDtypeStruct((2, width, half), low),
            jax.ShapeDtypeStruct((2, width, half), low),
            jax.ShapeDtypeStruct((2, half, width), low),
        ],
        in_specs=[anywhere] * 5,
        out_specs=[anywhere] * 5,
        scratch_shapes=[
            pltpu.VMEM((count, 2 * width), low),
            pltpu.VMEM((count, width + 128), low),
            pltpu.VMEM((width, units), low),
            pltpu.VMEM((width, units), low),
            pltpu.VMEM((units, width), low),
            pltpu.VMEM((count, units), low),
            pltpu.VMEM((count, units), low),
            pltpu.VMEM((count, units), low),
            pltpu.VMEM((width, units), low),
            pltpu.VMEM((width, units), low),
            pltpu.VMEM((units, width), low),
            pair, pair, pair, pair,
            pltpu.SemaphoreType.DMA((2,)),
            three, three, three, three, three,
        ],
        compiler_params=pltpu.CompilerParams(
            collective_id=1, has_side_effects=True, vmem_limit_bytes=60 * 2**20
        ),
    )(out_main, out_extra, *weights)


def body(
    tokens, cotangent, expert_ids, norm_gain, router_weight, gate_weight, up_weight, down_weight
):
    experts = router_weight.shape[1]
    rows_here, width = tokens.shape
    widened = tokens.astype(jnp.float32)
    inverse = lax.rsqrt(jnp.mean(widened * widened, axis=1, keepdims=True) + EPSILON)
    scaled = widened * inverse
    normed = (scaled * norm_gain).astype(jnp.bfloat16)
    logits = jnp.dot(normed, router_weight, preferred_element_type=jnp.float32)
    labels = jnp.arange(experts, dtype=jnp.int32)
    member = jnp.any(expert_ids[:, :, None] == labels, axis=1)
    lifted = jnp.where(member, jnp.exp(jnp.where(member, logits, 0.0)), 0.0)
    gates = lifted / jnp.sum(lifted, axis=1, keepdims=True)
    earlier = (
        jnp.arange(rows_here)[:, None] > jnp.arange(rows_here)[None, :]
    ).astype(jnp.bfloat16)
    rank = jnp.dot(earlier, member.astype(jnp.bfloat16), preferred_element_type=jnp.float32)
    rank = jnp.where(member, rank, -1.0).T

    def slots_of(first, count):
        block = jnp.repeat(rank, count, axis=0)
        slot = jnp.arange(experts * count, dtype=jnp.int32) % count + first
        return block == slot.astype(jnp.float32)[:, None]

    both = jnp.concatenate([normed, cotangent], axis=1)

    def dispatched(pick, slots):
        gate = jnp.sum(jnp.where(pick, jnp.repeat(gates.T, slots, axis=0), 0.0), axis=1)
        moved = jnp.dot(pick.astype(jnp.bfloat16), both, preferred_element_type=jnp.float32)
        is_upstream = jnp.arange(2 * width) >= width
        moved = moved * jnp.where(is_upstream[None, :], gate[:, None], 1.0)
        return moved.astype(jnp.bfloat16)

    picks = [slots_of(0, SLOTS), slots_of(SLOTS, EXTRA)]
    out_main = dispatched(picks[0], SLOTS)
    out_extra = dispatched(picks[1], EXTRA)
    picks = [pick.astype(jnp.bfloat16) for pick in picks]

    home_main, home_extra, *grads = moe(
        out_main, out_extra, (gate_weight, up_weight, down_weight)
    )

    def gathered(pick, home):
        return jnp.dot(
            jnp.concatenate([pick, pick]).T, home, preferred_element_type=jnp.float32
        )

    def scores(pick, home, slots):
        tail = jnp.sum(home[:, width:].astype(jnp.float32), axis=1, keepdims=True)
        tail = tail[: experts * slots] + tail[experts * slots :]
        return jnp.sum((pick * tail).reshape(experts, slots, rows_here), axis=1)

    total = gathered(picks[0], home_main) + gathered(picks[1], home_extra)
    grad_tok = total[:, :width]
    score_te = (scores(picks[0], home_main, SLOTS) + scores(picks[1], home_extra, EXTRA)).T
    grad_logits = (score_te - gates * jnp.sum(score_te, axis=1, keepdims=True)).astype(jnp.bfloat16)
    grad_normed = grad_tok + jnp.dot(
        grad_logits, router_weight.T, preferred_element_type=jnp.float32
    )
    router_part = jnp.dot(normed.T, grad_logits, preferred_element_type=jnp.float32)
    gain_part = jnp.sum(grad_normed * scaled, axis=0)
    sums = jnp.concatenate([router_part, gain_part[:, None]], axis=1)
    sums = sums.reshape(DEVICES, width // DEVICES, experts + 1)
    sums = lax.all_to_all(sums, ("dp", "ctx"), split_axis=0, concat_axis=0, tiled=True)
    sums = jnp.sum(sums, axis=0)
    grad_scaled = grad_normed * norm_gain
    correction = jnp.mean(grad_scaled * scaled, axis=1, keepdims=True)
    grad_input = (
        cotangent.astype(jnp.float32) + inverse * (grad_scaled - scaled * correction)
    ).astype(jnp.bfloat16)
    return (grad_input, *grads, sums[:, :experts], sums[:, experts])


def solution(mesh):
    return jax.shard_map(
        body,
        mesh=mesh,
        in_specs=(
            P(("dp", "ctx"), None),
            P(("dp", "ctx"), None),
            P(("dp", "ctx"), None),
            P(),
            P(),
            P("ctx", None, "dp"),
            P("ctx", None, "dp"),
            P("ctx", "dp", None),
        ),
        out_specs=(
            P(("dp", "ctx"), None),
            P("ctx", None, "dp"),
            P("ctx", None, "dp"),
            P("ctx", "dp", None),
            P(("dp", "ctx"), None),
            P(("dp", "ctx")),
        ),
        check_vma=False,
    )
```

time: 863 us -> 274 us (0.32)
  blocking collectives: 443 us -> 0 us
  Pallas kernels: 0 us -> 211 us
  waiting for transfers between devices: 122 us -> 12.4 us
  starting transfers between devices: 105 us -> 10.2 us
  matrix products: 105 us -> 11.9 us
  local copies, waits for them, and re-layouts: 48.2 us -> 15.7 us
  between operations: 14.4 us -> 0.94 us
    unnamed x2 -> x0, blocking collectives: 349 us -> none
    pallas_call x0 -> x1, Pallas kernels: none -> 211 us  [moe(): pl.pallas_call(moe_kernel, out_shape=[jax.ShapeDtypeStruct((DEVICES * SLO...]
    dot_general x12 -> x5, matrix products: 102 us -> 8.95 us  [the longest x2 4.48 us: gathered(): jnp.dot(jnp.concatenate([pick, pick]).T, home, preferred_element_type=jnp...]
    all_gather x2 -> x0, waiting for transfers between devices: 90.4 us -> none  [the longest x1 48.2 us: body(): lax.all_gather(arrived[1], 'dp', axis=2, tiled=True)]
    all_to_all x3 -> x0, blocking collectives: 81.9 us -> none  [the longest x1 38.7 us: body(): lax.all_to_all(out_rows, 'ctx', split_axis=0, concat_axis=2, tiled=True)]
    unnamed x17 -> x0, starting transfers between devices: 75.7 us -> none
    unnamed x21 -> x0, waiting for transfers between devices: 26.3 us -> none
    reshape x6 -> x0, local copies, waits for them, and re-layouts: 23.9 us -> none  [the longest x2 9.28 us: body(): out_grad = out_grad.reshape(ctx_size, local, capacity, width)]
  transfers between devices with their start and end apart: 22 -> 1, of which waited for: 4 -> 1; matrix products, arithmetic and copies ran while one was open for 43% -> 0% of each run, Pallas kernels for 0% -> 0%
where the time goes in v1:
time: 274 us
  Pallas kernels  211 us (77%)
  local copies, waits for them, and re-layouts  15.7 us (6%)
  waiting for transfers between devices  12.4 us (5%)
  matrix products  11.9 us (4%)
  other arithmetic  11.3 us (4%)
  starting transfers between devices  10.2 us (4%)
    pallas_call x1, Pallas kernels, moe(): pl.pallas_call(moe_kernel, out_shape=[jax.ShapeDtypeStruct((DEVICES * SLO...  211 us
    all_to_all x1, waiting for transfers between devices, body(): lax.all_to_all(sums, ('dp', 'ctx'), split_axis=0, concat_axis=0, tiled=True)  12.4 us
    unnamed x23, local copies, waits for them, and re-layouts  11.4 us
    all_to_all x1, starting transfers between devices, body(): lax.all_to_all(sums, ('dp', 'ctx'), split_axis=0, concat_axis=0, tiled=True)  10.2 us
  transfers between devices with their start and end apart: 1, of which 1 were waited for; matrix products, arithmetic and copies ran while one was open for 0% of the time, Pallas kernels for 0%

profile of v1, /device:TPU:1, one launch (start us, length us, event | category | flops | bytes accessed | tf_op | source)
XLA Modules:
  0.0 273.7 jit_solution(11453857579625547115)
XLA Ops:
  0.7 1.3 fusion.12
  2.0 0.7 fusion.18
  2.9 1.2 fusion.5
  4.1 0.3 fusion.37
  4.5 0.2 fusion.17
  4.8 0.2 fusion.23
  5.4 3.0 %multiply_convert_fusion.out_main = bf16[512,3584]{1,0:T(8,128)(2,1)} fusion(f32[512]{0:T(512)S(1)} %broadcast_in_dim.100, pred[3584]{0:T(1024)(128)(4,1)S(1)} %iota_compare_fusion.3, bf16[128,1792]{1,0:T(8,128)(2,1)S(1)} %copy-done.5, bf16[128,1792]{1,0:T(8,128)(2,1)S(1)} %fusion.5, f32[512]{0:T(512)S(1)} %fusion.38, f32[64,128]{1,0:T(8,128)S(1)} %convolution_select_fusion), kind=kOutput, calls=%fused_computation | convolution fusion | flops 477167616 | bytes 4627968 | tf_op jit(solution)/shard_map/dot_general | solution.py:310
  8.4 1.3 fusion.out_extra
  9.8 211.3 %shard_map.127 = (bf16[1024,1920]{1,0:T(8,128)(2,1)}, bf16[256,1920]{1,0:T(8,128)(2,1)}, bf16[2,1792,384]{2,1,0:T(8,128)(2,1)}, bf16[2,1792,384]{2,1,0:T(8,128)(2,1)}, bf16[2,384,1792]{2,1,0:T(8,128)(2,1)}) custom-call(bf16[512,3584]{1,0:T(8,128)(2,1)} %multiply_convert_fusion.out_main, bf16[128,3584]{1,0:T(8,128)(2,1)} %fusion.out_extra, ...), custom_call_target="tpu_custom_call" | custom-call | tf_op jit(solution)/shard_map/pallas_call | solution.py:248
  221.1 1.6 fusion.19
  222.6 0.9 convert_reduce_fusion.1
  223.6 1.1 convert_reduce_fusion
  224.7 2.9 %fusion.13 = f32[128,1920]{1,0:T(8,128)S(1)} fusion(bf16[1024,1920]{1,0:T(8,128)(2,1)} %get-tuple-element.11, pred[512,128]{1,0:T(32,128)(4,1)S(1)} %bitcast_compare_fusion), kind=kOutput, calls=%fused_computation.23 | convolution fusion | flops 503447552 | bytes 4980736 | tf_op jit(solution)/shard_map/dot_general | solution.py:325
  227.8 0.2 multiply_reduce_fusion.1
  228.1 0.2 multiply_reduce_fusion
  228.4 1.2 fusion.48
  229.6 1.4 fusion.11
  231.0 0.3 concatenate.31
  231.4 2.2 concatenate.28
  233.6 1.6 pad_maximum_fusion
  235.2 2.6 reshape.142
  237.8 10.2 %all-to-all-start = ((f32[128,1,910]{2,1,0:T(1,128)}), f32[128,1,910]{2,1,0:T(1,128)S(1)}, u32[]{:S(2)}, u32[]{:S(2)}) async-start(f32[128,1,910]{2,1,0:T(1,128)} %reshape.142), calls=%async_computation | async-start | bytes 1048576 | tf_op jit(solution)/shard_map/all_to_all | solution.py:345
  248.0 1.1 fusion.10
  249.2 12.4 %all-to-all-done = f32[128,1,910]{2,1,0:T(1,128)S(1)} async-done(((f32[128,1,910]{2,1,0:T(1,128)}), f32[128,1,910]{2,1,0:T(1,128)S(1)}, u32[]{:S(2)}, u32[]{:S(2)}) %all-to-all-start) | async-done | bytes 465952 | tf_op jit(solution)/shard_map/all_to_all | solution.py:345
  261.6 0.5 broadcast.113
  262.1 1.9 reduce.5
  264.0 0.7 reshape.143
  264.9 0.7 slice_reduce_fusion
  265.6 3.7 %copy.47 = bf16[2,1792,384]{2,1,0:T(8,128)(2,1)} copy(bf16[2,1792,384]{2,1,0:T(8,128)(2,1)} %get-tuple-element.28) | data formatting | bytes 5505024
  269.4 1.5 copy.48
  270.9 1.2 copy-done.3
  272.2 1.5 copy.49
  (38 shorter events, 1.2 us)
Async XLA Ops:
  0.6 3.5 %copy-start = (bf16[1792,64]{0,1:T(8,128)(2,1)S(1)}, bf16[1792,64]{0,1:T(8,128)(2,1)}, u32[]{:S(2)}) copy-start(bf16[1792,64]{0,1:T(8,128)(2,1)} %param.12) | copy-start | bytes 688132
  0.6 4.8 %copy-start.5 = (bf16[128,1792]{1,0:T(8,128)(2,1)S(1)}, bf16[128,1792]{1,0:T(8,128)(2,1)}, u32[]{:S(2)}) copy-start(bf16[128,1792]{1,0:T(8,128)(2,1)} %param.9) | copy-start | bytes 1376260
  224.7 4.9 %copy-start.1 = (bf16[128,1792]{1,0:T(8,128)(2,1)S(1)}, bf16[128,1792]{1,0:T(8,128)(2,1)}, u32[]{:S(2)}) copy-start(bf16[128,1792]{1,0:T(8,128)(2,1)} %param.8) | copy-start | bytes 1376260
  224.7 4.9 %copy-start.7 = (f32[1792]{0:T(1024)S(1)}, f32[1792]{0:T(1024)}, u32[]{:S(2)}) copy-start(f32[1792]{0:T(1024)} %param.11) | copy-start | bytes 21508
  233.6 14.4 %copy-start.6 = (bf16[128,1792]{1,0:T(8,128)(2,1)S(1)}, bf16[128,1792]{1,0:T(8,128)(2,1)}, u32[]{:S(2)}) copy-start(bf16[128,1792]{1,0:T(8,128)(2,1)} %param.9) | copy-start | bytes 1376260
  235.2 12.8 %copy-start.2 = (f32[128,1792]{1,0:T(8,128)S(1)}, f32[128,1792]{1,0:T(8,128)}, u32[]{:S(2)}) copy-start(f32[128,1792]{1,0:T(8,128)} %get-tuple-element.20) | copy-start | bytes 2752516
  237.8 23.8 %all-to-all-start = ((f32[128,1,910]{2,1,0:T(1,128)}), f32[128,1,910]{2,1,0:T(1,128)S(1)}, u32[]{:S(2)}, u32[]{:S(2)}) async-start(f32[128,1,910]{2,1,0:T(1,128)} %reshape.142), calls=%async_computation | async-start | bytes 1048576 | tf_op jit(solution)/shard_map/all_to_all | solution.py:345
  264.9 4.4 %copy-start.8 = (f32[14,65]{1,0:T(8,128)}, f32[14,65]{1,0:T(8,128)S(1)}, u32[]{:S(2)}) copy-start(f32[14,65]{1,0:T(8,128)S(1)} %reduce_sum.119) | copy-start | bytes 10924
  265.6 3.7 %copy-start.4 = (bf16[2,1792,384]{2,1,0:T(8,128)(2,1)S(1)}, bf16[2,1792,384]{2,1,0:T(8,128)(2,1)}, u32[]{:S(2)}) copy-start(bf16[2,1792,384]{2,1,0:T(8,128)(2,1)} %get-tuple-element.29) | copy-start | bytes 8257540
  269.4 2.8 %copy-start.3 = (bf16[2,384,1792]{2,1,0:T(8,128)(2,1)S(1)}, bf16[2,384,1792]{2,1,0:T(8,128)(2,1)}, u32[]{:S(2)}) copy-start(bf16[2,384,1792]{2,1,0:T(8,128)(2,1)} %get-tuple-element.30) | copy-start | bytes 8257540

commit v2 on v1

--- a/solution.py
+++ b/solution.py
@@ -39,10 +39,11 @@
 
 def moe_kernel(
     out_main, out_extra, gate_weight, up_weight, down_weight,
-    home_main, home_extra, gate_grad, up_grad, down_grad,
-    rows, back, w_gate, w_up, w_down, hid, gat, upp, gate_buf, up_buf, down_buf,
+    pick_main, pick_extra, gates, tokens, cotangent, norm_gain, router_weight,
+    grad_tokens, gate_grad, up_grad, down_grad, sums, bounce,
+    home_main, home_extra, part_sums, all_sums, rows, back, w_gate, w_up, w_down, hid, gat, upp, gate_buf, up_buf, down_buf,
     go_send, go_recv, home_send, home_recv, local_sem, load_sem,
-    weight_send, weight_recv, grad_send, grad_recv,
+    weight_send, weight_recv, grad_send, grad_recv, sum_send, sum_recv,
 ):
     x, y, z, core = coordinates()
     mine = device_of(x, y, z, core)
@@ -203,41 +204,129 @@
 
     lax.fori_loop(0, 1, units, 0)
     lax.fori_loop(1, DEVICES, return_extra, 0)
+    away = [
+        pltpu.make_async_copy(main_slot(back, 0), main_slot(bounce, 0), local_sem.at[0]),
+        pltpu.make_async_copy(extra_slot(back, 0, edge), extra_slot(bounce, 0, SLOTS), local_sem.at[1]),
+    ]
     kept = [
-        pltpu.make_async_copy(main_slot(back, 0), main_slot(home_main, own_index), local_sem.at[0]),
+        pltpu.make_async_copy(main_slot(bounce, 0), main_slot(home_main, own_index), local_sem.at[0]),
         pltpu.make_async_copy(
-            extra_slot(back, 0, edge), extra_slot(home_extra, own_index), local_sem.at[1]
+            extra_slot(bounce, 0, SLOTS), extra_slot(home_extra, own_index), local_sem.at[1]
         ),
     ]
+    for item in away:
+        item.start()
+    lax.fori_loop(1, 2 * half // TILE, units, 0)
+    for item in away:
+        item.wait()
     for item in kept:
         item.start()
-    lax.fori_loop(1, 2 * half // TILE, units, 0)
     lax.fori_loop(0, width // TILE, columns, 0)
     grads = zip((down_buf, gate_buf, up_buf), (down_grad, gate_grad, up_grad))
+    moves = []
     for i, (buf, out) in enumerate(grads):
-        kept.append(remote(part(buf, 1), out.at[core], grad_send.at[i], grad_recv.at[i], partner))
-        kept.append(pltpu.make_async_copy(part(buf, 0), out.at[core], load_sem.at[i]))
-    for item in kept[2:]:
+        moves.append(remote(part(buf, 1), out.at[core], grad_send.at[i], grad_recv.at[i], partner))
+        moves.append(pltpu.make_async_copy(part(buf, 0), out.at[core], load_sem.at[i]))
+    for item in moves:
         item.start()
 
-    def finish(k, carry):
+    def home_came(k, carry):
+        index = half_and_expert(*target(k))
+        for kind in range(2):
+            home_copy(k, source(k), index, kind).wait_recv()
+        return carry
+
+    lax.fori_loop(1, DEVICES, home_came, 0)
+    for item in kept:
+        item.wait()
+
+    low, high = jnp.bfloat16, jnp.float32
+    experts = router_weight.shape[1]
+    total, score = None, None
+    for pick, home, slots in ((pick_main, home_main, SLOTS), (pick_extra, home_extra, EXTRA)):
+        count = experts * slots
+        one_hot = pick[...]
+        tail = home[:, width:].astype(high)
+        tail = jnp.sum(tail[:count] + tail[count:], axis=1, keepdims=True)
+        spread = one_hot.astype(high) * tail
+        spread_high = spread.astype(low)
+        spread_low = (spread - spread_high.astype(high)).astype(low)
+        group = (
+            lax.broadcasted_iota(jnp.int32, (count, experts), 0) // slots
+            == lax.broadcasted_iota(jnp.int32, (count, experts), 1)
+        ).astype(low)
+        items = [
+            dot(spread_high, group, ((0,), (0,))),
+            dot(spread_low, group, ((0,), (0,))),
+        ]
+        score = sum(items) if score is None else score + sum(items)
+        both = dot(one_hot, home[:count, :width], ((0,), (0,)))
+        both = both + dot(one_hot, home[count:, :width], ((0,), (0,)))
+        total = both if total is None else total + both
+    grad_logits = (
+        score - gates[...] * jnp.sum(score, axis=1, keepdims=True)
+    ).astype(low)
+    grad_normed = total + dot(grad_logits, router_weight[...], ((1,), (1,)))
+    widened = tokens[...].astype(high)
+    inverse = lax.rsqrt(jnp.mean(widened * widened, axis=1, keepdims=True) + EPSILON)
+    scaled = widened * inverse
+    gained = (scaled * norm_gain[...]).astype(low)
+    gain = grad_normed * scaled
+    gain_high = gain.astype(low)
+    gain_low = (gain - gain_high.astype(high)).astype(low)
+    ones = jnp.ones((gain.shape[0], experts), low)
+    gain_sum = dot(gain_high, ones, ((0,), (0,))) + dot(gain_low, ones, ((0,), (0,)))
+    lane = lax.broadcasted_iota(jnp.int32, gain_sum.shape, 1)
+    sum_high = gain_sum.astype(low).astype(high)
+    gain_parts = jnp.where(lane == 0, sum_high, jnp.where(lane == 1, gain_sum - sum_high, 0.0))
+    router_part = dot(gained, grad_logits, ((0,), (0,)))
+    part = jnp.concatenate([router_part, gain_parts], axis=1).astype(low)
+    part_sums[...] = part.reshape(part_sums.shape)
+    grad_scaled = grad_normed * norm_gain[...]
+    correction = jnp.mean(grad_scaled * scaled, axis=1, keepdims=True)
+    grad_tokens[...] = (
+        cotangent[...].astype(high) + inverse * (grad_scaled - scaled * correction)
+    ).astype(low)
+
+    pairs = part_sums.shape[0] // DEVICES
+
+    def piece(k):
+        dp, ctx = target(k)
+        return remote(
+            part_sums.at[pl.ds((dp * 32 + ctx) * pairs, pairs)], all_sums.at[k],
+            sum_send.at[k], sum_recv.at[k], (dp, ctx),
+        )
+
+    def piece_go(k, carry):
+        piece(k).start()
+        return carry
+
+    lax.fori_loop(1, DEVICES, piece_go, 0)
+    all_sums[0] = part_sums[pl.ds((mine[0] * 32 + mine[1]) * pairs, pairs)]
+
+    def drain(k, carry):
         go_main(k).wait_send()
         go_extra(k).wait_send()
-        index = half_and_expert(*target(k))
         for kind in range(2):
             home_copy(k, source(k), own_index, kind).wait_send()
-            home_copy(k, source(k), index, kind).wait_recv()
-        return carry
-
-    lax.fori_loop(1, DEVICES, finish, 0)
-    for item in kept:
+        return carry
+
+    lax.fori_loop(1, DEVICES, drain, 0)
+    for item in moves:
         item.wait()
 
+    def piece_came(k, carry):
+        piece(k).wait()
+        return carry
+
+    lax.fori_loop(1, DEVICES, piece_came, 0)
+    sums[...] = jnp.sum(all_sums[...].astype(high), axis=0)
+
 
 TILE = 256
 
 
-def moe(out_main, out_extra, weights):
+def moe(out_main, out_extra, weights, local):
     half, width = weights[2].shape[1:]
     units = 2 * half
     count = DEVICES * (SLOTS + EXTRA)
@@ -245,18 +334,26 @@
     anywhere = pl.BlockSpec(memory_space=pl.ANY)
     pair = pltpu.SemaphoreType.DMA((2, DEVICES))
     three = pltpu.SemaphoreType.DMA((3,))
+    each = pltpu.SemaphoreType.DMA((DEVICES,))
+    vmem = pl.BlockSpec(memory_space=pltpu.VMEM)
+    pairs = width // (2 * DEVICES)
     return pl.pallas_call(
         moe_kernel,
         out_shape=[
-            jax.ShapeDtypeStruct((DEVICES * SLOTS, width + 128), low),
-            jax.ShapeDtypeStruct((DEVICES * EXTRA, width + 128), low),
+            jax.ShapeDtypeStruct(local[3].shape, low),
             jax.ShapeDtypeStruct((2, width, half), low),
             jax.ShapeDtypeStruct((2, width, half), low),
             jax.ShapeDtypeStruct((2, half, width), low),
+            jax.ShapeDtypeStruct((pairs, 2, 128), jnp.float32),
+            jax.ShapeDtypeStruct((2 * SLOTS, width + 128), low),
         ],
-        in_specs=[anywhere] * 5,
-        out_specs=[anywhere] * 5,
+        in_specs=[anywhere] * 5 + [vmem] * 7,
+        out_specs=[vmem] + [anywhere] * 3 + [vmem, anywhere],
         scratch_shapes=[
+            pltpu.VMEM((DEVICES * SLOTS, width + 128), low),
+            pltpu.VMEM((DEVICES * EXTRA, width + 128), low),
+            pltpu.VMEM((DEVICES * pairs, 2, 128), low),
+            pltpu.VMEM((DEVICES, pairs, 2, 128), low),
             pltpu.VMEM((count, 2 * width), low),
             pltpu.VMEM((count, width + 128), low),
             pltpu.VMEM((width, units), low),
@@ -271,11 +368,12 @@
             pair, pair, pair, pair,
             pltpu.SemaphoreType.DMA((2,)),
             three, three, three, three, three,
+            each, each,
         ],
         compiler_params=pltpu.CompilerParams(
             collective_id=1, has_side_effects=True, vmem_limit_bytes=60 * 2**20
         ),
-    )(out_main, out_extra, *weights)
+    )(out_main, out_extra, *weights, *local)
 
 
 def body(
@@ -317,39 +415,14 @@
     out_extra = dispatched(picks[1], EXTRA)
     picks = [pick.astype(jnp.bfloat16) for pick in picks]
 
-    home_main, home_extra, *grads = moe(
-        out_main, out_extra, (gate_weight, up_weight, down_weight)
+    grad_tokens, *grads, sums, _ = moe(
+        out_main,
+        out_extra,
+        (gate_weight, up_weight, down_weight),
+        (*picks, gates, tokens, cotangent, norm_gain[None, :], router_weight),
     )
-
-    def gathered(pick, home):
-        return jnp.dot(
-            jnp.concatenate([pick, pick]).T, home, preferred_element_type=jnp.float32
-        )
-
-    def scores(pick, home, slots):
-        tail = jnp.sum(home[:, width:].astype(jnp.float32), axis=1, keepdims=True)
-        tail = tail[: experts * slots] + tail[experts * slots :]
-        return jnp.sum((pick * tail).reshape(experts, slots, rows_here), axis=1)
-
-    total = gathered(picks[0], home_main) + gathered(picks[1], home_extra)
-    grad_tok = total[:, :width]
-    score_te = (scores(picks[0], home_main, SLOTS) + scores(picks[1], home_extra, EXTRA)).T
-    grad_logits = (score_te - gates * jnp.sum(score_te, axis=1, keepdims=True)).astype(jnp.bfloat16)
-    grad_normed = grad_tok + jnp.dot(
-        grad_logits, router_weight.T, preferred_element_type=jnp.float32
-    )
-    router_part = jnp.dot(normed.T, grad_logits, preferred_element_type=jnp.float32)
-    gain_part = jnp.sum(grad_normed * scaled, axis=0)
-    sums = jnp.concatenate([router_part, gain_part[:, None]], axis=1)
-    sums = sums.reshape(DEVICES, width // DEVICES, experts + 1)
-    sums = lax.all_to_all(sums, ("dp", "ctx"), split_axis=0, concat_axis=0, tiled=True)
-    sums = jnp.sum(sums, axis=0)
-    grad_scaled = grad_normed * norm_gain
-    correction = jnp.mean(grad_scaled * scaled, axis=1, keepdims=True)
-    grad_input = (
-        cotangent.astype(jnp.float32) + inverse * (grad_scaled - scaled * correction)
-    ).astype(jnp.bfloat16)
-    return (grad_input, *grads, sums[:, :experts], sums[:, experts])
+    sums = sums.reshape(width // DEVICES, 128)
+    return (grad_tokens, *grads, sums[:, :experts], sums[:, experts] + sums[:, experts + 1])
 
 
 def solution(mesh):

time: 274 us -> 259 us (0.945)
  Pallas kernels: 211 us -> 232 us
  waiting for transfers between devices: 12.4 us -> 0 us
  starting transfers between devices: 10.2 us -> 0 us
  matrix products: 11.9 us -> 5.62 us
  other arithmetic: 11.3 us -> 6.72 us
    pallas_call x1, Pallas kernels: 211 us -> 232 us  [moe(): pl.pallas_call(moe_kernel, out_shape=[jax.ShapeDtypeStruct(local[3].shape...]
    all_to_all x1 -> x0, waiting for transfers between devices: 12.4 us -> none  [body(): lax.all_to_all(sums, ('dp', 'ctx'), split_axis=0, concat_axis=0, tiled=True)]
    all_to_all x1 -> x0, starting transfers between devices: 10.2 us -> none  [body(): lax.all_to_all(sums, ('dp', 'ctx'), split_axis=0, concat_axis=0, tiled=True)]
    dot_general x4 -> x0, matrix products: 7.1 us -> none  [the longest x2 4.48 us: gathered(): jnp.dot(jnp.concatenate([pick, pick]).T, home, preferred_element_type=jnp...]
    unnamed x23 -> x15, local copies, waits for them, and re-layouts: 11.4 us -> 10.9 us
  transfers between devices with their start and end apart: 1 -> 0, of which waited for: 1 -> 0; matrix products, arithmetic and copies ran while one was open for 0% -> 0% of each run, Pallas kernels for 0% -> 0%
where the time goes in v2:
time: 259 us; the launch traced here: 258 us
  Pallas kernels  232 us (90%)
  local copies, waits for them, and re-layouts  13.3 us (5%)
  other arithmetic  6.72 us (3%)
  matrix products  5.62 us (2%)
    pallas_call x1, Pallas kernels, moe(): pl.pallas_call(moe_kernel, out_shape=[jax.ShapeDtypeStruct(local[3].shape...  232 us
    unnamed x15, local copies, waits for them, and re-layouts  10.9 us

profile of v2, /device:TPU:1, one launch (start us, length us, event | category | flops | bytes accessed | tf_op | source)
XLA Modules:
  0.0 258.2 jit_solution(11324831289420098491)
XLA Ops:
  0.6 0.0 copy-start.3
  0.6 0.0 copy-start.2
  0.7 1.3 fusion.1
  2.0 1.3 broadcast_in_dim.107.norm_gain
  3.3 0.7 fusion.7
  4.0 0.1 copy.34
  4.1 0.1 convolution_select_fusion
  4.3 0.7 fusion.32
  5.0 0.8 fusion.4.pick_main
  5.8 1.2 fusion.3
  7.0 1.2 fusion.33
  8.2 0.1 copy.33
  8.3 0.1 fusion.10
  8.4 0.7 fusion.9.gates
  9.2 0.2 fusion.8
  9.4 0.2 select_reduce_fusion
  9.7 0.1 broadcast_in_dim.104
  9.8 0.1 broadcast_in_dim.97
  9.9 0.0 copy-done.2
  9.9 1.0 copy.35.router_weight
  10.9 0.0 copy-done.3
  10.9 1.3 fusion.out_extra
  12.2 3.0 %multiply_convert_fusion.out_main = bf16[512,3584]{1,0:T(8,128)(2,1)} fusion(f32[512]{0:T(512)S(1)} %broadcast_in_dim.97, pred[3584]{0:T(1024)(128)(4,1)S(1)} %iota_compare_fusion.3, bf16[128,1792]{1,0:T(8,128)(2,1)S(1)} %copy-done.3, bf16[128,1792]{1,0:T(8,128)(2,1)S(1)} %fusion.3, f32[512]{0:T(512)S(1)} %fusion.24, f32[64,128]{1,0:T(8,128)S(1)} %convolution_select_fusion), kind=kOutput, calls=%fused_computation | convolution fusion | flops 477167616 | bytes 4627968 | tf_op jit(solution)/shard_map/dot_general | solution.py:408
  15.2 231.8 %shard_map.127 = (bf16[128,1792]{1,0:T(8,128)(2,1)}, bf16[2,1792,384]{2,1,0:T(8,128)(2,1)}, bf16[2,1792,384]{2,1,0:T(8,128)(2,1)}, bf16[2,384,1792]{2,1,0:T(8,12...) custom-call(bf16[512,3584]{1,0:T(8,128)(2,1)} %multiply_convert_fusion.out_main, ...), custom_call_target="tpu_custom_call" | custom-call | tf_op jit(solution)/shard_map/pallas_call | solution.py:340
  246.9 0.7 reshape.80
  247.6 0.7 fusion.23
  248.3 1.8 copy.42
  250.1 3.7 %copy.43 = bf16[2,1792,384]{2,1,0:T(8,128)(2,1)} copy(bf16[2,1792,384]{2,1,0:T(8,128)(2,1)} %get-tuple-element.25) | data formatting | bytes 5505024
  253.9 0.0 copy-done.1
  253.9 1.5 copy.44
  255.4 1.2 copy-done
  256.7 1.5 copy.45
  (12 shorter events, 0.1 us)
Async XLA Ops:
  0.6 10.2 %copy-start.3 = (bf16[128,1792]{1,0:T(8,128)(2,1)S(1)}, bf16[128,1792]{1,0:T(8,128)(2,1)}, u32[]{:S(2)}) copy-start(bf16[128,1792]{1,0:T(8,128)(2,1)} %cotangent.1) | copy-start | bytes 1376260
  0.6 9.2 %copy-start.2 = (bf16[1792,64]{0,1:T(8,128)(2,1)S(1)}, bf16[1792,64]{0,1:T(8,128)(2,1)}, u32[]{:S(2)}) copy-start(bf16[1792,64]{0,1:T(8,128)(2,1)} %param.12) | copy-start | bytes 688132
  247.6 6.3 %copy-start.4 = (f32[14,128]{1,0:T(8,128)}, f32[14,128]{1,0:T(8,128)S(1)}, u32[]{:S(2)}) copy-start(f32[14,128]{1,0:T(8,128)S(1)} %reshape.80) | copy-start | bytes 21508
  250.1 3.7 %copy-start.1 = (bf16[2,1792,384]{2,1,0:T(8,128)(2,1)S(1)}, bf16[2,1792,384]{2,1,0:T(8,128)(2,1)}, u32[]{:S(2)}) copy-start(bf16[2,1792,384]{2,1,0:T(8,128)(2,1)} %get-tuple-element.26) | copy-start | bytes 8257540
  253.9 2.8 %copy-start = (bf16[2,384,1792]{2,1,0:T(8,128)(2,1)S(1)}, bf16[2,384,1792]{2,1,0:T(8,128)(2,1)}, u32[]{:S(2)}) copy-start(bf16[2,384,1792]{2,1,0:T(8,128)(2,1)} %get-tuple-element.27) | copy-start | bytes 8257540

commit v3 on v2

--- a/solution.py
+++ b/solution.py
@@ -38,10 +38,10 @@
 
 
 def moe_kernel(
-    out_main, out_extra, gate_weight, up_weight, down_weight,
-    pick_main, pick_extra, gates, tokens, cotangent, norm_gain, router_weight,
+    gate_weight, up_weight, down_weight,
+    tokens, cotangent, expert_ids, norm_gain, router_weight,
     grad_tokens, gate_grad, up_grad, down_grad, sums, bounce,
-    home_main, home_extra, part_sums, all_sums, rows, back, w_gate, w_up, w_down, hid, gat, upp, gate_buf, up_buf, down_buf,
+    out_main, out_extra, pick_main, pick_extra, gates, home_main, home_extra, part_sums, all_sums, rows, back, w_gate, w_up, w_down, hid, gat, upp, gate_buf, up_buf, down_buf,
     go_send, go_recv, home_send, home_recv, local_sem, load_sem,
     weight_send, weight_recv, grad_send, grad_recv, sum_send, sum_recv,
 ):
@@ -80,6 +80,66 @@
         return carry
 
     lax.fori_loop(1, DEVICES, greet, 0)
+
+    low, high = jnp.bfloat16, jnp.float32
+    experts = router_weight.shape[1]
+    tokens_here = tokens.shape[0]
+    places = (w_gate, w_up, w_down)
+
+    def part(buf, i):
+        at = pl.ds(i * half, half)
+        return buf.at[at] if buf.shape[0] == 2 * half else buf.at[:, at]
+
+    loads = [
+        pltpu.make_async_copy(weight.at[core], part(place, 0), load_sem.at[i])
+        for i, (weight, place) in enumerate(zip((gate_weight, up_weight, down_weight), places))
+    ]
+    for item in loads:
+        item.start()
+
+    def iota(shape, dim):
+        return lax.broadcasted_iota(jnp.int32, shape, dim)
+
+    def normalized():
+        widened = tokens[...].astype(high)
+        inverse = lax.rsqrt(jnp.mean(widened * widened, axis=1, keepdims=True) + EPSILON)
+        scaled = widened * inverse
+        return inverse, scaled, (scaled * norm_gain[...]).astype(low)
+
+    normed_here = normalized()[2]
+    logits = dot(normed_here, router_weight[...], ((1,), (0,)))
+    label = iota((tokens_here, experts), 1)
+    ids = expert_ids[...]
+    member = ids[:, 0:1] == label
+    for k in range(1, ids.shape[1]):
+        member = member | (ids[:, k : k + 1] == label)
+    lifted = jnp.where(member, jnp.exp(jnp.where(member, logits, 0.0)), 0.0)
+    gate = lifted / jnp.sum(lifted, axis=1, keepdims=True)
+    gates[...] = gate
+    gate_high = gate.astype(low)
+    gate_low = (gate - gate_high.astype(high)).astype(low)
+    earlier = iota((tokens_here, tokens_here), 0) > iota((tokens_here, tokens_here), 1)
+    named = member.astype(high).astype(low)
+    rank = dot(earlier.astype(high).astype(low), named, ((1,), (0,)))
+    rank = jnp.where(member, rank, -1.0).astype(low)
+    for out, chosen, slots, first in (
+        (out_main, pick_main, SLOTS, 0), (out_extra, pick_extra, EXTRA, SLOTS)
+    ):
+        count = experts * slots
+        spread = (iota((experts, count), 1) // slots == iota((experts, count), 0))
+        spread = spread.astype(high).astype(low)
+        slot = (iota((tokens_here, count), 1) % slots + first).astype(high)
+        hit = dot(rank, spread, ((1,), (0,))) == slot
+        one_hot = hit.astype(high).astype(low)
+        chosen[...] = one_hot
+        out[:, :width] = dot(one_hot, normed_here, ((0,), (0,))).astype(low)
+        scaled_up = None
+        for piece_of in (gate_high, gate_low):
+            weighted = jnp.where(hit, dot(piece_of, spread, ((1,), (0,))), 0.0).astype(low)
+            term = dot(weighted, cotangent[...], ((0,), (0,)))
+            scaled_up = term if scaled_up is None else scaled_up + term
+        out[:, width:] = scaled_up.astype(low)
+
     pl.semaphore_wait(barrier, DEVICES - 1)
 
     def remote(src, dst, send, recv, device):
@@ -119,33 +179,35 @@
         home_copy(k, source(k), own_index, 1).start()
         return carry
 
-    places = (w_gate, w_up, w_down)
-
-    def part(buf, i):
-        at = pl.ds(i * half, half)
-        return buf.at[at] if buf.shape[0] == 2 * half else buf.at[:, at]
-
-    loads = []
-    for i, (weight, place) in enumerate(zip((gate_weight, up_weight, down_weight), places)):
-        loads.append(remote(
-            weight.at[1 - core], part(place, 1), weight_send.at[i], weight_recv.at[i], partner
-        ))
-        loads.append(pltpu.make_async_copy(weight.at[core], part(place, 0), load_sem.at[i]))
+    swaps = [
+        remote(weight.at[1 - core], part(place, 1), weight_send.at[i], weight_recv.at[i], partner)
+        for i, (weight, place) in enumerate(zip((gate_weight, up_weight, down_weight), places))
+    ]
     own = expert_of(*mine)
-    loads.append(pltpu.make_async_copy(main_slot(out_main, own), main_slot(rows, 0), local_sem.at[0]))
-    loads.append(
-        pltpu.make_async_copy(extra_slot(out_extra, own), extra_slot(rows, 0, edge), local_sem.at[1])
-    )
+    leave = [
+        pltpu.make_async_copy(main_slot(out_main, own), main_slot(bounce, 0), local_sem.at[0]),
+        pltpu.make_async_copy(extra_slot(out_extra, own), extra_slot(bounce, 0, SLOTS), local_sem.at[1]),
+    ]
+    enter = [
+        pltpu.make_async_copy(main_slot(bounce, 0), main_slot(rows, 0), local_sem.at[0]),
+        pltpu.make_async_copy(
+            extra_slot(bounce, 0, SLOTS), extra_slot(rows, 0, edge), local_sem.at[1]
+        ),
+    ]
 
     def go(k, carry):
         go_main(k).start()
         go_extra(k).start()
         return carry
 
-    for item in loads:
-        item.start()
     lax.fori_loop(1, DEVICES, go, 0)
-    for item in loads:
+    for item in swaps + leave:
+        item.start()
+    for item in leave:
+        item.wait()
+    for item in enter:
+        item.start()
+    for item in loads + swaps + enter:
         item.wait()
 
     def main_came(k, carry):
@@ -204,14 +266,16 @@
 
     lax.fori_loop(0, 1, units, 0)
     lax.fori_loop(1, DEVICES, return_extra, 0)
+    lanes = back.shape[1]
+    near = bounce.at[:, pl.ds(0, lanes)]
     away = [
-        pltpu.make_async_copy(main_slot(back, 0), main_slot(bounce, 0), local_sem.at[0]),
-        pltpu.make_async_copy(extra_slot(back, 0, edge), extra_slot(bounce, 0, SLOTS), local_sem.at[1]),
+        pltpu.make_async_copy(main_slot(back, 0), main_slot(near, 0), local_sem.at[0]),
+        pltpu.make_async_copy(extra_slot(back, 0, edge), extra_slot(near, 0, SLOTS), local_sem.at[1]),
     ]
     kept = [
-        pltpu.make_async_copy(main_slot(bounce, 0), main_slot(home_main, own_index), local_sem.at[0]),
+        pltpu.make_async_copy(main_slot(near, 0), main_slot(home_main, own_index), local_sem.at[0]),
         pltpu.make_async_copy(
-            extra_slot(bounce, 0, SLOTS), extra_slot(home_extra, own_index), local_sem.at[1]
+            extra_slot(near, 0, SLOTS), extra_slot(home_extra, own_index), local_sem.at[1]
         ),
     ]
     for item in away:
@@ -240,43 +304,32 @@
     for item in kept:
         item.wait()
 
-    low, high = jnp.bfloat16, jnp.float32
-    experts = router_weight.shape[1]
     total, score = None, None
     for pick, home, slots in ((pick_main, home_main, SLOTS), (pick_extra, home_extra, EXTRA)):
         count = experts * slots
         one_hot = pick[...]
         tail = home[:, width:].astype(high)
         tail = jnp.sum(tail[:count] + tail[count:], axis=1, keepdims=True)
-        spread = one_hot.astype(high) * tail
+        group = iota((count, experts), 0) // slots == iota((count, experts), 1)
+        spread = jnp.where(group, tail, 0.0)
         spread_high = spread.astype(low)
         spread_low = (spread - spread_high.astype(high)).astype(low)
-        group = (
-            lax.broadcasted_iota(jnp.int32, (count, experts), 0) // slots
-            == lax.broadcasted_iota(jnp.int32, (count, experts), 1)
-        ).astype(low)
-        items = [
-            dot(spread_high, group, ((0,), (0,))),
-            dot(spread_low, group, ((0,), (0,))),
-        ]
-        score = sum(items) if score is None else score + sum(items)
-        both = dot(one_hot, home[:count, :width], ((0,), (0,)))
-        both = both + dot(one_hot, home[count:, :width], ((0,), (0,)))
+        here = dot(one_hot, spread_high, ((1,), (0,))) + dot(one_hot, spread_low, ((1,), (0,)))
+        score = here if score is None else score + here
+        both = dot(one_hot, home[:count, :width], ((1,), (0,)))
+        both = both + dot(one_hot, home[count:, :width], ((1,), (0,)))
         total = both if total is None else total + both
     grad_logits = (
         score - gates[...] * jnp.sum(score, axis=1, keepdims=True)
     ).astype(low)
     grad_normed = total + dot(grad_logits, router_weight[...], ((1,), (1,)))
-    widened = tokens[...].astype(high)
-    inverse = lax.rsqrt(jnp.mean(widened * widened, axis=1, keepdims=True) + EPSILON)
-    scaled = widened * inverse
-    gained = (scaled * norm_gain[...]).astype(low)
+    inverse, scaled, gained = normalized()
     gain = grad_normed * scaled
     gain_high = gain.astype(low)
     gain_low = (gain - gain_high.astype(high)).astype(low)
     ones = jnp.ones((gain.shape[0], experts), low)
     gain_sum = dot(gain_high, ones, ((0,), (0,))) + dot(gain_low, ones, ((0,), (0,)))
-    lane = lax.broadcasted_iota(jnp.int32, gain_sum.shape, 1)
+    lane = iota(gain_sum.shape, 1)
     sum_high = gain_sum.astype(low).astype(high)
     gain_parts = jnp.where(lane == 0, sum_high, jnp.where(lane == 1, gain_sum - sum_high, 0.0))
     router_part = dot(gained, grad_logits, ((0,), (0,)))
@@ -326,7 +379,7 @@
 TILE = 256
 
 
-def moe(out_main, out_extra, weights, local):
+def moe(weights, local):
     half, width = weights[2].shape[1:]
     units = 2 * half
     count = DEVICES * (SLOTS + EXTRA)
@@ -337,19 +390,25 @@
     each = pltpu.SemaphoreType.DMA((DEVICES,))
     vmem = pl.BlockSpec(memory_space=pltpu.VMEM)
     pairs = width // (2 * DEVICES)
+    here, experts = local[0].shape[0], local[4].shape[1]
     return pl.pallas_call(
         moe_kernel,
         out_shape=[
-            jax.ShapeDtypeStruct(local[3].shape, low),
+            jax.ShapeDtypeStruct(local[0].shape, low),
             jax.ShapeDtypeStruct((2, width, half), low),
             jax.ShapeDtypeStruct((2, width, half), low),
             jax.ShapeDtypeStruct((2, half, width), low),
             jax.ShapeDtypeStruct((pairs, 2, 128), jnp.float32),
-            jax.ShapeDtypeStruct((2 * SLOTS, width + 128), low),
+            jax.ShapeDtypeStruct((2 * SLOTS, 2 * width), low),
         ],
-        in_specs=[anywhere] * 5 + [vmem] * 7,
+        in_specs=[anywhere] * 3 + [vmem] * 5,
         out_specs=[vmem] + [anywhere] * 3 + [vmem, anywhere],
         scratch_shapes=[
+            pltpu.VMEM((experts * SLOTS, 2 * width), low),
+            pltpu.VMEM((experts * EXTRA, 2 * width), low),
+            pltpu.VMEM((here, experts * SLOTS), low),
+            pltpu.VMEM((here, experts * EXTRA), low),
+            pltpu.VMEM((here, experts), jnp.float32),
             pltpu.VMEM((DEVICES * SLOTS, width + 128), low),
             pltpu.VMEM((DEVICES * EXTRA, width + 128), low),
             pltpu.VMEM((DEVICES * pairs, 2, 128), low),
@@ -373,53 +432,17 @@
         compiler_params=pltpu.CompilerParams(
             collective_id=1, has_side_effects=True, vmem_limit_bytes=60 * 2**20
         ),
-    )(out_main, out_extra, *weights, *local)
+    )(*weights, *local)
 
 
 def body(
     tokens, cotangent, expert_ids, norm_gain, router_weight, gate_weight, up_weight, down_weight
 ):
     experts = router_weight.shape[1]
-    rows_here, width = tokens.shape
-    widened = tokens.astype(jnp.float32)
-    inverse = lax.rsqrt(jnp.mean(widened * widened, axis=1, keepdims=True) + EPSILON)
-    scaled = widened * inverse
-    normed = (scaled * norm_gain).astype(jnp.bfloat16)
-    logits = jnp.dot(normed, router_weight, preferred_element_type=jnp.float32)
-    labels = jnp.arange(experts, dtype=jnp.int32)
-    member = jnp.any(expert_ids[:, :, None] == labels, axis=1)
-    lifted = jnp.where(member, jnp.exp(jnp.where(member, logits, 0.0)), 0.0)
-    gates = lifted / jnp.sum(lifted, axis=1, keepdims=True)
-    earlier = (
-        jnp.arange(rows_here)[:, None] > jnp.arange(rows_here)[None, :]
-    ).astype(jnp.bfloat16)
-    rank = jnp.dot(earlier, member.astype(jnp.bfloat16), preferred_element_type=jnp.float32)
-    rank = jnp.where(member, rank, -1.0).T
-
-    def slots_of(first, count):
-        block = jnp.repeat(rank, count, axis=0)
-        slot = jnp.arange(experts * count, dtype=jnp.int32) % count + first
-        return block == slot.astype(jnp.float32)[:, None]
-
-    both = jnp.concatenate([normed, cotangent], axis=1)
-
-    def dispatched(pick, slots):
-        gate = jnp.sum(jnp.where(pick, jnp.repeat(gates.T, slots, axis=0), 0.0), axis=1)
-        moved = jnp.dot(pick.astype(jnp.bfloat16), both, preferred_element_type=jnp.float32)
-        is_upstream = jnp.arange(2 * width) >= width
-        moved = moved * jnp.where(is_upstream[None, :], gate[:, None], 1.0)
-        return moved.astype(jnp.bfloat16)
-
-    picks = [slots_of(0, SLOTS), slots_of(SLOTS, EXTRA)]
-    out_main = dispatched(picks[0], SLOTS)
-    out_extra = dispatched(picks[1], EXTRA)
-    picks = [pick.astype(jnp.bfloat16) for pick in picks]
-
+    width = tokens.shape[1]
     grad_tokens, *grads, sums, _ = moe(
-        out_main,
-        out_extra,
         (gate_weight, up_weight, down_weight),
-        (*picks, gates, tokens, cotangent, norm_gain[None, :], router_weight),
+        (tokens, cotangent, expert_ids, norm_gain[None, :], router_weight),
     )
     sums = sums.reshape(width // DEVICES, 128)
     return (grad_tokens, *grads, sums[:, :experts], sums[:, experts] + sums[:, experts + 1])

time: 259 us -> 248 us (0.958)
  other arithmetic: 6.72 us -> 0.7 us
  matrix products: 5.62 us -> 0 us
    dot_general x4 -> x0, matrix products: 5.62 us -> none  [the longest x2 4.28 us: dispatched(): jnp.dot(pick.astype(jnp.bfloat16), both, preferred_element_type=jnp.float32)]
    convert_element_type x7 -> x0, other arithmetic: 2.73 us -> none  [the longest x2 1.48 us: dispatched(): pick.astype(jnp.bfloat16)]
    unnamed x15 -> x12, local copies, waits for them, and re-layouts: 10.9 us -> 13.2 us
where the time goes in v3:
time: 248 us
  Pallas kernels  231 us (93%)
  local copies, waits for them, and re-layouts  15.2 us (6%)
    pallas_call x1, Pallas kernels, moe(): pl.pallas_call(moe_kernel, out_shape=[jax.ShapeDtypeStruct(local[0].shape...  231 us
    unnamed x12, local copies, waits for them, and re-layouts  13.2 us

profile of v3, /device:TPU:1, one launch (start us, length us, event | category | flops | bytes accessed | tf_op | source)
XLA Modules:
  0.0 247.8 jit_solution(5493396564367456878)
XLA Ops:
  0.6 1.4 copy.16.expert_ids
  2.0 1.3 broadcast_in_dim.3.norm_gain
  3.3 1.9 copy.17.router_weight
  5.3 231.3 %shard_map.127 = (bf16[128,1792]{1,0:T(8,128)(2,1)}, bf16[2,1792,384]{2,1,0:T(8,128)(2,1)}, bf16[2,1792,384]{2,1,0:T(8,128)(2,1)}, bf16[2,384,1792]{2,1,0:T(8,12...) custom-call(bf16[2,1792,384]{2,1,0:T(8,128)(2,1)} %gate_weight.1, bf16[2,1792,384]{2,1,0:T(8,128)(2,1)} %up_weight.1, ...), custom_call_target="tpu_custom_call" | custom-call | tf_op jit(solution)/shard_map/pallas_call | solution.py:394
  236.6 0.7 reshape.16
  237.3 0.0 copy-start.2
  237.3 0.7 fusion
  238.0 1.8 copy.22
  239.8 0.0 copy-start.1
  239.8 3.7 %copy.23 = bf16[2,1792,384]{2,1,0:T(8,128)(2,1)} copy(bf16[2,1792,384]{2,1,0:T(8,128)(2,1)} %get-tuple-element.23) | data formatting | bytes 5505024
  243.5 0.0 copy-done.2
  243.5 0.0 copy-done.1
  243.5 0.0 copy-start
  243.5 1.5 copy.24
  245.1 1.2 copy-done
  246.3 1.5 copy.25
Async XLA Ops:
  237.3 6.3 %copy-start.2 = (f32[14,128]{1,0:T(8,128)}, f32[14,128]{1,0:T(8,128)S(1)}, u32[]{:S(2)}) copy-start(f32[14,128]{1,0:T(8,128)S(1)} %reshape.16) | copy-start | bytes 21508
  239.8 3.7 %copy-start.1 = (bf16[2,1792,384]{2,1,0:T(8,128)(2,1)S(1)}, bf16[2,1792,384]{2,1,0:T(8,128)(2,1)}, u32[]{:S(2)}) copy-start(bf16[2,1792,384]{2,1,0:T(8,128)(2,1)} %get-tuple-element.24) | copy-start | bytes 8257540
  243.5 2.8 %copy-start = (bf16[2,384,1792]{2,1,0:T(8,128)(2,1)S(1)}, bf16[2,384,1792]{2,1,0:T(8,128)(2,1)}, u32[]{:S(2)}) copy-start(bf16[2,384,1792]{2,1,0:T(8,128)(2,1)} %get-tuple-element.25) | copy-start | bytes 8257540

commit v4 on v3

--- a/solution.py
+++ b/solution.py
@@ -82,7 +82,7 @@
     lax.fori_loop(1, DEVICES, greet, 0)
 
     low, high = jnp.bfloat16, jnp.float32
-    experts = router_weight.shape[1]
+    experts = router_weight.shape[0]
     tokens_here = tokens.shape[0]
     places = (w_gate, w_up, w_down)
 
@@ -100,37 +100,44 @@
     def iota(shape, dim):
         return lax.broadcasted_iota(jnp.int32, shape, dim)
 
+    def as_low(flag):
+        return flag.astype(high).astype(low)
+
+    gain_row = jnp.concatenate([norm_gain[i : i + 1, :] for i in range(width // 128)], axis=1)
+
     def normalized():
         widened = tokens[...].astype(high)
         inverse = lax.rsqrt(jnp.mean(widened * widened, axis=1, keepdims=True) + EPSILON)
         scaled = widened * inverse
-        return inverse, scaled, (scaled * norm_gain[...]).astype(low)
+        return inverse, scaled, (scaled * gain_row).astype(low)
 
     normed_here = normalized()[2]
-    logits = dot(normed_here, router_weight[...], ((1,), (0,)))
-    label = iota((tokens_here, experts), 1)
+    logits = dot(normed_here, router_weight[...], ((1,), (1,)))
+    label = iota((experts, tokens_here), 0)
     ids = expert_ids[...]
-    member = ids[:, 0:1] == label
-    for k in range(1, ids.shape[1]):
-        member = member | (ids[:, k : k + 1] == label)
+    turned = ids[0:1] == label
+    for k in range(1, ids.shape[0]):
+        turned = turned | (ids[k : k + 1] == label)
+    same = iota((experts, experts), 0) == iota((experts, experts), 1)
+    member = dot(as_low(turned), as_low(same), ((0,), (0,))) > 0.5
     lifted = jnp.where(member, jnp.exp(jnp.where(member, logits, 0.0)), 0.0)
     gate = lifted / jnp.sum(lifted, axis=1, keepdims=True)
     gates[...] = gate
     gate_high = gate.astype(low)
     gate_low = (gate - gate_high.astype(high)).astype(low)
     earlier = iota((tokens_here, tokens_here), 0) > iota((tokens_here, tokens_here), 1)
-    named = member.astype(high).astype(low)
-    rank = dot(earlier.astype(high).astype(low), named, ((1,), (0,)))
+    named = as_low(member)
+    rank = dot(as_low(earlier), named, ((1,), (0,)))
     rank = jnp.where(member, rank, -1.0).astype(low)
     for out, chosen, slots, first in (
         (out_main, pick_main, SLOTS, 0), (out_extra, pick_extra, EXTRA, SLOTS)
     ):
         count = experts * slots
         spread = (iota((experts, count), 1) // slots == iota((experts, count), 0))
-        spread = spread.astype(high).astype(low)
+        spread = as_low(spread)
         slot = (iota((tokens_here, count), 1) % slots + first).astype(high)
         hit = dot(rank, spread, ((1,), (0,))) == slot
-        one_hot = hit.astype(high).astype(low)
+        one_hot = as_low(hit)
         chosen[...] = one_hot
         out[:, :width] = dot(one_hot, normed_here, ((0,), (0,))).astype(low)
         scaled_up = None
@@ -322,7 +329,7 @@
     grad_logits = (
         score - gates[...] * jnp.sum(score, axis=1, keepdims=True)
     ).astype(low)
-    grad_normed = total + dot(grad_logits, router_weight[...], ((1,), (1,)))
+    grad_normed = total + dot(grad_logits, router_weight[...], ((1,), (0,)))
     inverse, scaled, gained = normalized()
     gain = grad_normed * scaled
     gain_high = gain.astype(low)
@@ -335,7 +342,7 @@
     router_part = dot(gained, grad_logits, ((0,), (0,)))
     part = jnp.concatenate([router_part, gain_parts], axis=1).astype(low)
     part_sums[...] = part.reshape(part_sums.shape)
-    grad_scaled = grad_normed * norm_gain[...]
+    grad_scaled = grad_normed * gain_row
     correction = jnp.mean(grad_scaled * scaled, axis=1, keepdims=True)
     grad_tokens[...] = (
         cotangent[...].astype(high) + inverse * (grad_scaled - scaled * correction)
@@ -390,7 +397,7 @@
     each = pltpu.SemaphoreType.DMA((DEVICES,))
     vmem = pl.BlockSpec(memory_space=pltpu.VMEM)
     pairs = width // (2 * DEVICES)
-    here, experts = local[0].shape[0], local[4].shape[1]
+    here, experts = local[0].shape[0], local[4].shape[0]
     return pl.pallas_call(
         moe_kernel,
         out_shape=[
@@ -435,6 +442,36 @@
     )(*weights, *local)
 
 
+def settle_kernel(*refs):
+    count = (len(refs) - 2) // 3
+    ins, outs, held = refs[:count], refs[count : 2 * count], refs[2 * count : 3 * count]
+    in_sem, out_sem = refs[3 * count :]
+    takes = [pltpu.make_async_copy(a, b, in_sem.at[i]) for i, (a, b) in enumerate(zip(ins, held))]
+    gives = [pltpu.make_async_copy(a, b, out_sem.at[i]) for i, (a, b) in enumerate(zip(held, outs))]
+    for item in takes:
+        item.start()
+    for take, give in zip(takes, gives):
+        take.wait()
+        give.start()
+    for item in gives:
+        item.wait()
+
+
+def settle(arrays):
+    anywhere = pl.BlockSpec(memory_space=pl.ANY)
+    count = len(arrays)
+    return pl.pallas_call(
+        settle_kernel,
+        out_shape=[jax.ShapeDtypeStruct(a.shape, a.dtype) for a in arrays],
+        in_specs=[anywhere] * count,
+        out_specs=[anywhere] * count,
+        scratch_shapes=[pltpu.VMEM(a.shape, a.dtype) for a in arrays]
+        + [pltpu.SemaphoreType.DMA((count,)), pltpu.SemaphoreType.DMA((count,))],
+        compiler_params=pltpu.CompilerParams(vmem_limit_bytes=60 * 2**20),
+        cost_estimate=pl.CostEstimate(flops=10**6, bytes_accessed=17 * 2**20, transcendentals=0),
+    )(*arrays)
+
+
 def body(
     tokens, cotangent, expert_ids, norm_gain, router_weight, gate_weight, up_weight, down_weight
 ):
@@ -442,9 +479,10 @@
     width = tokens.shape[1]
     grad_tokens, *grads, sums, _ = moe(
         (gate_weight, up_weight, down_weight),
-        (tokens, cotangent, expert_ids, norm_gain[None, :], router_weight),
+        (tokens, cotangent, expert_ids.T, norm_gain.reshape(width // 128, 128), router_weight.T),
     )
     sums = sums.reshape(width // DEVICES, 128)
+    grad_tokens, *grads = settle([grad_tokens, *grads])
     return (grad_tokens, *grads, sums[:, :experts], sums[:, experts] + sums[:, experts + 1])
 
 

time: 248 us -> 235 us (0.948)
  local copies, waits for them, and re-layouts: 15.2 us -> 0.02 us
  Pallas kernels: 231 us -> 234 us
    unnamed x12 -> x4, local copies, waits for them, and re-layouts: 13.2 us -> 0.01 us
    pallas_call x0 -> x1, Pallas kernels: none -> 7.26 us  [settle(): pl.pallas_call(settle_kernel, out_shape=[jax.ShapeDtypeStruct(a.shape, a....]
    pallas_call x1, Pallas kernels: 231 us -> 227 us  [moe(): pl.pallas_call(moe_kernel, out_shape=[jax.ShapeDtypeStruct(local[0].shape...]
where the time goes in v4:
time: 235 us
  Pallas kernels  234 us (100%)
    pallas_call x1, Pallas kernels, moe(): pl.pallas_call(moe_kernel, out_shape=[jax.ShapeDtypeStruct(local[0].shape...  227 us
    pallas_call x1, Pallas kernels, settle(): pl.pallas_call(settle_kernel, out_shape=[jax.ShapeDtypeStruct(a.shape, a....  7.26 us

profile of v4, /device:TPU:1, one launch (start us, length us, event | category | flops | bytes accessed | tf_op | source)
XLA Modules:
  0.0 235.3 jit_solution(15802931928996727239)
XLA Ops:
  0.6 226.7 %shard_map.127 = (bf16[128,1792]{1,0:T(8,128)(2,1)}, bf16[2,1792,384]{2,1,0:T(8,128)(2,1)}, bf16[2,1792,384]{2,1,0:T(8,128)(2,1)}, bf16[2,384,1792]{2,1,0:T(8,12...) custom-call(bf16[2,1792,384]{2,1,0:T(8,128)(2,1)} %gate_weight.1, bf16[2,1792,384]{2,1,0:T(8,128)(2,1)} %up_weight.1, ...), custom_call_target="tpu_custom_call" | custom-call | tf_op jit(solution)/shard_map/pallas_call | solution.py:401
  227.3 0.0 copy-start.1
  227.3 7.3 %shard_map.128 = (bf16[128,1792]{1,0:T(8,128)(2,1)}, bf16[2,1792,384]{2,1,0:T(8,128)(2,1)}, bf16[2,1792,384]{2,1,0:T(8,128)(2,1)}, bf16[2,384,1792]{2,1,0:T(8,128)(2,1)}) custom-call(bf16[128,1792]{1,0:T(8,128)(2,1)} %get-tuple-element.15.refs_0_, bf16[2,1792,384]{2,1,0:T(8,128)(2,1)} %get-tuple-element.16.refs_1_, ...), custom_call_target="tpu_custom_call" | custom-call | flops 1000000 | bytes 17825792 | tf_op jit(solution)/shard_map/pallas_call | solution.py:463
  234.6 0.0 copy-done.1
  234.6 0.0 copy-start
  234.6 0.7 fusion
  235.3 0.0 copy-done
  (1 shorter events, 0.0 us)
Async XLA Ops:
  227.3 7.3 %copy-start.1 = (f32[7,2,128]{2,1,0:T(2,128)S(1)}, f32[7,2,128]{2,1,0:T(2,128)}, u32[]{:S(2)}) copy-start(f32[7,2,128]{2,1,0:T(2,128)} %get-tuple-element.23) | copy-start | bytes 21508
  234.6 0.7 copy-start

commit v5 on v4

--- a/solution.py
+++ b/solution.py
@@ -54,17 +54,17 @@
 
     def turn(k, sign, flip):
         return device_of(
-            (x + sign * k + DEVICES) % 4,
-            (y + sign * (3 * k + k // 4) + 4 * DEVICES) % 4,
-            (z + sign * (2 * k + k // 4 + k // 16) + 4 * DEVICES) % 4,
+            (x + sign * (2 * k + k // 4) + 4 * DEVICES) % 4,
+            (y + sign * k + 4 * DEVICES) % 4,
+            (z + sign * (3 * k + k // 4 + k // 16) + 4 * DEVICES) % 4,
             flip,
         )
 
     def target(k):
-        return turn(k, 1 - 2 * core, (core + k // 64 + k // 4) % 2)
+        return turn(k, 1 - 2 * core, (core + k // 64 + k // 16) % 2)
 
     def source(k):
-        other = (core + k // 64 + k // 4) % 2
+        other = (core + k // 64 + k // 16) % 2
         return turn(k, 2 * other - 1, other)
 
     def main_slot(ref, i):

time: 235 us -> 233 us (level); the launches traced: 235 us -> 231 us
  Pallas kernels: 234 us -> 229 us
    pallas_call x1, Pallas kernels: 227 us -> 222 us  [moe(): pl.pallas_call(moe_kernel, out_shape=[jax.ShapeDtypeStruct(local[0].shape...]
where the time goes in v5:
time: 233 us; the launch traced here: 231 us
  Pallas kernels  229 us (98%)
    pallas_call x1, Pallas kernels, moe(): pl.pallas_call(moe_kernel, out_shape=[jax.ShapeDtypeStruct(local[0].shape...  222 us
    pallas_call x1, Pallas kernels, settle(): pl.pallas_call(settle_kernel, out_shape=[jax.ShapeDtypeStruct(a.shape, a....  7.26 us

profile of v5, /device:TPU:1, one launch (start us, length us, event | category | flops | bytes accessed | tf_op | source)
XLA Modules:
  0.0 230.6 jit_solution(6874591374842162365)
XLA Ops:
  0.6 221.9 %shard_map.127 = (bf16[128,1792]{1,0:T(8,128)(2,1)}, bf16[2,1792,384]{2,1,0:T(8,128)(2,1)}, bf16[2,1792,384]{2,1,0:T(8,128)(2,1)}, bf16[2,384,1792]{2,1,0:T(8,12...) custom-call(bf16[2,1792,384]{2,1,0:T(8,128)(2,1)} %gate_weight.1, bf16[2,1792,384]{2,1,0:T(8,128)(2,1)} %up_weight.1, ...), custom_call_target="tpu_custom_call" | custom-call | tf_op jit(solution)/shard_map/pallas_call | solution.py:401
  222.6 0.0 copy-start.1
  222.6 7.3 %shard_map.128 = (bf16[128,1792]{1,0:T(8,128)(2,1)}, bf16[2,1792,384]{2,1,0:T(8,128)(2,1)}, bf16[2,1792,384]{2,1,0:T(8,128)(2,1)}, bf16[2,384,1792]{2,1,0:T(8,128)(2,1)}) custom-call(bf16[128,1792]{1,0:T(8,128)(2,1)} %get-tuple-element.15.refs_0_, bf16[2,1792,384]{2,1,0:T(8,128)(2,1)} %get-tuple-element.16.refs_1_, ...), custom_call_target="tpu_custom_call" | custom-call | flops 1000000 | bytes 17825792 | tf_op jit(solution)/shard_map/pallas_call | solution.py:463
  229.9 0.0 copy-done.1
  229.9 0.0 copy-start
  229.9 0.7 fusion
  230.6 0.0 copy-done
  (1 shorter events, 0.0 us)
Async XLA Ops:
  222.6 7.3 %copy-start.1 = (f32[7,2,128]{2,1,0:T(2,128)S(1)}, f32[7,2,128]{2,1,0:T(2,128)}, u32[]{:S(2)}) copy-start(f32[7,2,128]{2,1,0:T(2,128)} %get-tuple-element.23) | copy-start | bytes 21508
  229.9 0.7 copy-start

commit v6 on v5

--- a/solution.py
+++ b/solution.py
@@ -55,7 +55,7 @@
     def turn(k, sign, flip):
         return device_of(
             (x + sign * (2 * k + k // 4) + 4 * DEVICES) % 4,
-            (y + sign * k + 4 * DEVICES) % 4,
+            (y - sign * k + 4 * DEVICES) % 4,
             (z + sign * (3 * k + k // 4 + k // 16) + 4 * DEVICES) % 4,
             flip,
         )

time: 233 us -> 241 us (1.034)
  Pallas kernels: 229 us -> 239 us
    pallas_call x1, Pallas kernels: 222 us -> 232 us  [moe(): pl.pallas_call(moe_kernel, out_shape=[jax.ShapeDtypeStruct(local[0].shape...]
where the time goes in v6:
time: 241 us; the launch traced here: 240 us
  Pallas kernels  239 us (99%)
    pallas_call x1, Pallas kernels, moe(): pl.pallas_call(moe_kernel, out_shape=[jax.ShapeDtypeStruct(local[0].shape...  232 us
    pallas_call x1, Pallas kernels, settle(): pl.pallas_call(settle_kernel, out_shape=[jax.ShapeDtypeStruct(a.shape, a....  7.26 us

profile of v6, /device:TPU:1, one launch (start us, length us, event | category | flops | bytes accessed | tf_op | source)
XLA Modules:
  0.0 240.5 jit_solution(1131835994025803237)
XLA Ops:
  0.6 231.8 %shard_map.127 = (bf16[128,1792]{1,0:T(8,128)(2,1)}, bf16[2,1792,384]{2,1,0:T(8,128)(2,1)}, bf16[2,1792,384]{2,1,0:T(8,128)(2,1)}, bf16[2,384,1792]{2,1,0:T(8,12...) custom-call(bf16[2,1792,384]{2,1,0:T(8,128)(2,1)} %gate_weight.1, bf16[2,1792,384]{2,1,0:T(8,128)(2,1)} %up_weight.1, ...), custom_call_target="tpu_custom_call" | custom-call | tf_op jit(solution)/shard_map/pallas_call | solution.py:401
  232.4 0.0 copy-start.1
  232.4 7.3 %shard_map.128 = (bf16[128,1792]{1,0:T(8,128)(2,1)}, bf16[2,1792,384]{2,1,0:T(8,128)(2,1)}, bf16[2,1792,384]{2,1,0:T(8,128)(2,1)}, bf16[2,384,1792]{2,1,0:T(8,128)(2,1)}) custom-call(bf16[128,1792]{1,0:T(8,128)(2,1)} %get-tuple-element.15.refs_0_, bf16[2,1792,384]{2,1,0:T(8,128)(2,1)} %get-tuple-element.16.refs_1_, ...), custom_call_target="tpu_custom_call" | custom-call | flops 1000000 | bytes 17825792 | tf_op jit(solution)/shard_map/pallas_call | solution.py:463
  239.7 0.0 copy-done.1
  239.7 0.0 copy-start
  239.8 0.7 fusion
  240.5 0.0 copy-done
  (1 shorter events, 0.0 us)
Async XLA Ops:
  232.4 7.3 %copy-start.1 = (f32[7,2,128]{2,1,0:T(2,128)S(1)}, f32[7,2,128]{2,1,0:T(2,128)}, u32[]{:S(2)}) copy-start(f32[7,2,128]{2,1,0:T(2,128)} %get-tuple-element.23) | copy-start | bytes 21508
  239.7 0.7 copy-start
